TPU v7x, 8 devices: a whole 2x2x1 slice. The times are simulated.
8 devices in a mesh: dp: 2 (over z, y), ctx: 4 (over x, core).
Axes of the slice: x: 2, y: 2, z: 1, core: 2. Of those that a mesh axis runs over, the one named last changes fastest.
Arguments:
- x_chunk: bfloat16 [6144, 2048], P(('dp', 'ctx')), parts along dimension 0
- cache_len: int32 [2], P('dp'), parts along dimension 0
- k_cache: bfloat16 [2, 16384, 16, 128], P(None, ('dp', 'ctx')), parts along dimension 1
- v_cache: bfloat16 [2, 16384, 16, 128], P(None, ('dp', 'ctx')), parts along dimension 1
- k_local: bfloat16 [2, 512, 16, 128], P(None, 'dp'), parts along dimension 1
- v_local: bfloat16 [2, 512, 16, 128], P(None, 'dp'), parts along dimension 1
- g_attn: bfloat16 [4, 2048], replicated
- g_mlp: bfloat16 [4, 2048], replicated
- w_q: bfloat16 [4, 2048, 2048], replicated
- w_k: bfloat16 [4, 2048, 2048], replicated
- w_v: bfloat16 [4, 2048, 2048], replicated
- w_o: bfloat16 [4, 2048, 2048], replicated
- w_gate: bfloat16 [4, 2048, 8192], replicated
- w_up: bfloat16 [4, 2048, 8192], replicated
- w_down: bfloat16 [4, 8192, 2048], replicated
Outputs:
- output: bfloat16 [6144, 2048], P(('dp', 'ctx')), parts along dimension 0
There are 2 independent parts. A program takes and returns all parts, laid end to end along the dimension named above; an argument that names none is the same for every part.
All inputs are finite; a program needn't handle non-finite values.
Results may differ from a plain program's by a relative error of at most 0.02.
Values are sent between devices in bfloat16 or wider.
A program may use at most 2.25 GiB of HBM per device.

v0:
```python
import functools

import jax
import jax.numpy as jnp
from jax import lax
from jax.experimental import pallas as pl
from jax.experimental.pallas import tpu as pltpu
from jax.sharding import PartitionSpec as P


NORM_EPS = 1e-6
HEAD_DIM = 128
LOG2E = 1.4426950408889634
EXP_SCALE = LOG2E * HEAD_DIM ** -0.5
BLOCK_K = 1024
NT = (((1,), (1,)), ((), ()))
TN = (((0,), (0,)), ((), ()))
ANY = pl.BlockSpec(memory_space=pl.ANY)


def rms_norm(rows_in, gain_vec):
    rows_f32 = rows_in.astype(jnp.float32)
    inv_rms = lax.rsqrt(jnp.mean(rows_f32 * rows_f32, axis=-1, keepdims=True) + NORM_EPS)
    return (rows_f32 * inv_rms * gain_vec.astype(jnp.float32)).astype(jnp.bfloat16)


def project(rows_in, weight):
    return jnp.dot(rows_in, weight, preferred_element_type=jnp.float32).astype(jnp.bfloat16)


def mlp_block(hidden, gain_vec, w_gate, w_up, w_down):
    normed = rms_norm(hidden, gain_vec)
    gate_pre = jnp.dot(normed, w_gate, preferred_element_type=jnp.float32)
    up_pre = jnp.dot(normed, w_up, preferred_element_type=jnp.float32)
    act_bf16 = (jax.nn.gelu(gate_pre, approximate=True) * up_pre).astype(jnp.bfloat16)
    return (hidden.astype(jnp.float32) + jnp.dot(act_bf16, w_down, preferred_element_type=jnp.float32)).astype(jnp.bfloat16)


def relay_kernel(me_ref, x_ref, *rest):
    outs, heads_s = rest[:-1], rest[-1]
    n_dev = len(outs)
    group = heads_s.shape[0] // n_dev
    me = me_ref[0]
    heads_s[...] = jnp.swapaxes(x_ref[...], 0, 1)
    for r, out in enumerate(outs):
        out[...] = heads_s[pl.ds(group * (me ^ r), group)]


def relay(me, cache, pair_idx, n_dev):
    _, slots, heads, dim = cache.shape
    rows = 512
    group = heads // n_dev
    return pl.pallas_call(
        relay_kernel,
        grid_spec=pltpu.PrefetchScalarGridSpec(
            num_scalar_prefetch=1,
            grid=(slots // rows,),
            in_specs=[pl.BlockSpec((None, rows, heads, dim), lambda i, m: (pair_idx, i, 0, 0))],
            out_specs=[pl.BlockSpec((group, rows, dim), lambda i, m: (0, i, 0))] * n_dev,
            scratch_shapes=[pltpu.VMEM((heads, rows, dim), cache.dtype)],
        ),
        out_shape=[jax.ShapeDtypeStruct((group, slots, dim), cache.dtype)] * n_dev,
        compiler_params=pltpu.CompilerParams(vmem_limit_bytes=40 << 20),
        cost_estimate=pl.CostEstimate(flops=0, bytes_accessed=4 * slots * heads * dim, transcendentals=0),
        name="cache_relay",
    )(me, cache)


def qkv_kernel(me_ref, h0_ref, h1_ref, wq_ref, wk_ref, wv_ref, q_ref, k_ref, v_ref):
    n_rows = h0_ref.shape[0]
    step = pl.program_id(0)
    for t, (w_ref, o_ref) in enumerate(((wq_ref, q_ref), (wk_ref, k_ref), (wv_ref, v_ref))):
        @pl.when(step // 2 == t)
        def _():
            for i, h_ref in enumerate((h0_ref, h1_ref)):
                o_ref[pl.ds(i * n_rows, n_rows), :] = jnp.dot(h_ref[...], w_ref[...], preferred_element_type=jnp.float32).astype(jnp.bfloat16)


def group_qkv(me, h0, h1, w_q, w_k, w_v, layer, n_dev):
    n_rows, depth = h0.shape
    group = w_q.shape[-1] // n_dev
    half = group // 2
    whole = pl.BlockSpec((n_rows, depth), lambda i, m: (0, 0))

    def w_spec(t):
        return pl.BlockSpec((None, depth, half), lambda i, m: (layer, 0, 2 * m[0] + jnp.clip(i - 2 * t, 0, 1)))

    def o_spec(t):
        return pl.BlockSpec((2 * n_rows, half), lambda i, m: (0, jnp.clip(i - 2 * t, 0, 1)))

    return pl.pallas_call(
        qkv_kernel,
        grid_spec=pltpu.PrefetchScalarGridSpec(
            num_scalar_prefetch=1,
            grid=(6,),
            in_specs=[whole, whole] + [w_spec(t) for t in range(3)],
            out_specs=[o_spec(t) for t in range(3)],
        ),
        out_shape=[jax.ShapeDtypeStruct((2 * n_rows, group), jnp.bfloat16)] * 3,
        compiler_params=pltpu.CompilerParams(vmem_limit_bytes=48 << 20),
        cost_estimate=pl.CostEstimate(flops=12 * n_rows * depth * group, bytes_accessed=4 * n_rows * depth + 6 * depth * group, transcendentals=0),
        name="group_qkv",
    )(me, h0, h1, w_q, w_k, w_v)


def out_kernel(me_ref, x_ref, o0, o1, o2, o3, w0, w1, w2, w3, y_ref):
    total = jnp.dot(o0[...], w0[...], preferred_element_type=jnp.float32)
    for o, w in ((o1, w1), (o2, w2), (o3, w3)):
        total = total + jnp.dot(o[...], w[...], preferred_element_type=jnp.float32)
    y_ref[...] = (x_ref[...].astype(jnp.float32) + total).astype(jnp.bfloat16)


def group_out(me, x, parts, w_o, layer):
    n_rows, width = x.shape
    group = parts[0].shape[1]
    cols = 512
    col_spec = pl.BlockSpec((n_rows, cols), lambda n, m: (0, n))
    part_spec = pl.BlockSpec((n_rows, group), lambda n, m: (0, 0))

    def w_spec(r):
        return pl.BlockSpec((None, group, cols), lambda n, m: (layer, m[0] ^ r, n))

    return pl.pallas_call(
        out_kernel,
        grid_spec=pltpu.PrefetchScalarGridSpec(
            num_scalar_prefetch=1,
            grid=(width // cols,),
            in_specs=[col_spec] + [part_spec] * 4 + [w_spec(r) for r in range(4)],
            out_specs=col_spec,
        ),
        out_shape=jax.ShapeDtypeStruct((n_rows, width), jnp.bfloat16),
        compiler_params=pltpu.CompilerParams(vmem_limit_bytes=48 << 20),
        cost_estimate=pl.CostEstimate(flops=2 * n_rows * width * width, bytes_accessed=2 * width * width, transcendentals=0),
        name="group_out",
    )(me, x, *parts, *([w_o] * 4))


def global_kernel(info_ref, q_ref, *rest, n_dev, slots, n_rows, first, use_cache, use_new, load, store):
    rest = list(rest)
    ck, cv = [[rest.pop(0) for _ in range(n_dev)] for _ in range(2)] if use_cache else ([], [])
    nk, nv = [[rest.pop(0) for _ in range(2)] for _ in range(2)] if use_new else ([], [])
    if load:
        m_in, l_in, acc_in = [rest.pop(0) for _ in range(3)]
    if store:
        m_out, l_out, acc_out = [rest.pop(0) for _ in range(3)]
    else:
        outs = [rest.pop(0) for _ in range(2)]
    kbuf, vbuf, s0, s1, qt, m_s, l_s, acc_s, sems = rest
    head, qi = pl.program_id(0), pl.program_id(1)
    n_heads = pl.num_programs(0)
    me, cache_len = info_ref[0], info_ref[1]
    n_cache = n_dev * slots if use_cache else 0

    def copies(h, slot):
        out = []
        col = pl.multiple_of(h * HEAD_DIM, HEAD_DIM)
        for t, (pieces, new, buf) in enumerate(((ck, nk, kbuf), (cv, nv, vbuf))):
            for r, piece in enumerate(pieces):
                dst = pl.multiple_of((me ^ r) * slots, slots)
                out.append(pltpu.make_async_copy(piece.at[h], buf.at[slot, pl.ds(dst, slots)], sems.at[slot, t, r]))
            for r in range(4 if use_new else 0):
                src = new[r // 2].at[pl.ds(n_rows * (r % 2), n_rows), pl.ds(col, HEAD_DIM)]
                dst = pl.multiple_of(n_cache + (me ^ r) * n_rows, 256)
                out.append(pltpu.make_async_copy(src, buf.at[slot, pl.ds(dst, n_rows)], sems.at[slot, t, n_dev + r]))
        return out

    slot = lax.rem(head, 2)

    @pl.when(qi == 0)
    def _():
        @pl.when(head == 0)
        def _():
            for c in copies(0, 0):
                c.start()

        @pl.when(head + 1 < n_heads)
        def _():
            for c in copies(head + 1, 1 - slot):
                c.start()

        for c in copies(head, slot):
            c.wait()

    qt[...] = q_ref[...].T
    if load:
        m_s[...], l_s[...], acc_s[...] = m_in[...], l_in[...], acc_in[...]
    else:
        m_s[...] = jnp.full_like(m_s, -jnp.inf)
        l_s[...] = jnp.zeros_like(l_s)
        acc_s[...] = jnp.zeros_like(acc_s)

    def scores(base, size):
        return jnp.dot(kbuf[slot, pl.ds(base, size), :], qt[...], preferred_element_type=jnp.float32)

    def update(base, s):
        size = s.shape[0]
        m_old = m_s[...]
        m_new = jnp.maximum(m_old, jnp.max(s, axis=0, keepdims=True))
        alpha = jnp.exp2((m_old - m_new) * EXP_SCALE)
        probs = jnp.exp2((s - m_new) * EXP_SCALE)
        l_s[...] = l_s[...] * alpha + jnp.sum(probs, axis=0, keepdims=True)
        weighted = lax.dot_general(vbuf[slot, pl.ds(base, size), :], probs.astype(jnp.bfloat16), TN, preferred_element_type=jnp.float32)
        acc_s[...] = acc_s[...] * alpha + weighted
        m_s[...] = m_new

    if use_cache:
        last = n_cache // BLOCK_K - 1
        n_full = cache_len // BLOCK_K
        n_left = cache_len - n_full * BLOCK_K

        def base_of(j):
            return pl.multiple_of(jnp.minimum(j, last) * BLOCK_K, BLOCK_K)

        def update_last(s):
            ids = lax.broadcasted_iota(jnp.int32, s.shape, 0)
            update(base_of(n_full), jnp.where(ids < n_left, s, -jnp.inf))

        s0[...] = scores(0, BLOCK_K)

        def pair(i, carry):
            j = 2 * i
            s1[...] = scores(base_of(j + 1), BLOCK_K)
            update(base_of(j), s0[...])
            s0[...] = scores(base_of(j + 2), BLOCK_K)
            update(base_of(j + 1), s1[...])
            return carry

        lax.fori_loop(0, n_full // 2, pair, 0)
        odd = lax.rem(n_full, 2) == 1

        @pl.when(odd)
        def _():
            s1[...] = scores(base_of(n_full), BLOCK_K)
            update(base_of(n_full - 1), s0[...])

            @pl.when(n_left > 0)
            def _():
                update_last(s1[...])

        @pl.when(jnp.logical_not(odd) & (n_left > 0))
        def _():
            update_last(s0[...])

    if use_new:
        piece = me ^ (first + qi)

        def new_base(j):
            return pl.multiple_of(n_cache + j * n_rows, 256)

        def earlier(j, carry):
            update(new_base(j), scores(new_base(j), n_rows))
            return carry

        lax.fori_loop(0, piece, earlier, 0)
        s = scores(new_base(piece), n_rows)
        key_ids = lax.broadcasted_iota(jnp.int32, s.shape, 0)
        row_ids = lax.broadcasted_iota(jnp.int32, s.shape, 1)
        update(new_base(piece), jnp.where(key_ids <= row_ids, s, -jnp.inf))

    if store:
        m_out[...], l_out[...], acc_out[...] = m_s[...], l_s[...], acc_s[...]
    else:
        result = (acc_s[...] / l_s[...]).T.astype(jnp.bfloat16)
        for i, o_ref in enumerate(outs):
            @pl.when(qi == i)
            def _():
                o_ref[...] = result


def global_attention(info, q, cache_k=(), cache_v=(), new_k=(), new_v=(), state=(), first=0, store=False, n_dev=4):
    dim = HEAD_DIM
    n_rows, group = q.shape[0] // 2, q.shape[1]
    heads = group // dim
    slots = cache_k[0].shape[1] if cache_k else 0
    n_keys = n_dev * (slots + (n_rows if new_k else 0))
    elems = heads * 2 * n_rows * (n_dev * slots * 3 // 4 + (n_dev * n_rows // 2 if new_k else 0))
    state_specs = [pl.BlockSpec((None, None, r, n_rows), lambda h, i, m: (h, i, 0, 0)) for r in (1, 1, dim)]
    state_shape = [jax.ShapeDtypeStruct((heads, 2, r, n_rows), jnp.float32) for r in (1, 1, dim)]
    return pl.pallas_call(
        functools.partial(global_kernel, n_dev=n_dev, slots=slots, n_rows=n_rows, first=first, use_cache=bool(cache_k), use_new=bool(new_k), load=bool(state), store=store),
        grid_spec=pltpu.PrefetchScalarGridSpec(
            num_scalar_prefetch=1,
            grid=(heads, 2),
            in_specs=[pl.BlockSpec((n_rows, dim), lambda h, i, m: (i, h))] + [ANY] * (2 * len(cache_k) + 2 * len(new_k)) + (state_specs if state else []),
            out_specs=state_specs if store else [pl.BlockSpec((n_rows, dim), lambda h, i, m: (0, h))] * 2,
            scratch_shapes=[
                pltpu.VMEM((2, n_keys, dim), jnp.bfloat16),
                pltpu.VMEM((2, n_keys, dim), jnp.bfloat16),
                pltpu.VMEM((BLOCK_K, n_rows), jnp.float32),
                pltpu.VMEM((BLOCK_K, n_rows), jnp.float32),
                pltpu.VMEM((dim, n_rows), jnp.bfloat16),
                pltpu.VMEM((1, n_rows), jnp.float32),
                pltpu.VMEM((1, n_rows), jnp.float32),
                pltpu.VMEM((dim, n_rows), jnp.float32),
                pltpu.SemaphoreType.DMA((2, 2, n_dev + 4)),
            ],
        ),
        out_shape=state_shape if store else [jax.ShapeDtypeStruct((n_rows, group), jnp.bfloat16)] * 2,
        compiler_params=pltpu.CompilerParams(vmem_limit_bytes=56 << 20),
        cost_estimate=pl.CostEstimate(flops=8 * elems * dim, bytes_accessed=4 * heads * n_keys * dim, transcendentals=elems),
        name="global_attention",
    )(info, q, *cache_k, *cache_v, *new_k, *new_v, *state)


def local_kernel(q_ref, k_ref, v_ref, hk_ref, hv_ref, o_ref, kbuf, vbuf, *, window):
    n_rows = q_ref.shape[0]
    dim = HEAD_DIM
    key_ids = lax.broadcasted_iota(jnp.int32, (2 * window, window), 0)
    row_ids = lax.broadcasted_iota(jnp.int32, (2 * window, window), 1)
    allowed = (key_ids > row_ids) & (key_ids <= row_ids + window)
    kbuf[pl.ds(0, window), :] = hk_ref[...]
    kbuf[pl.ds(window, n_rows), :] = k_ref[...]
    vbuf[pl.ds(0, window), :] = hv_ref[...]
    vbuf[pl.ds(window, n_rows), :] = v_ref[...]
    for h in range(q_ref.shape[1] // dim):
        cols = pl.ds(h * dim, dim)
        for b in range(n_rows // window):
            keys = pl.ds(b * window, 2 * window)
            rows = pl.ds(b * window, window)
            s = lax.dot_general(kbuf[keys, cols], q_ref[rows, cols], NT, preferred_element_type=jnp.float32)
            s = jnp.where(allowed, s, -jnp.inf)
            probs = jnp.exp2((s - jnp.max(s, axis=0, keepdims=True)) * EXP_SCALE)
            total = jnp.sum(probs, axis=0, keepdims=True)
            o = lax.dot_general(vbuf[keys, cols], probs.astype(jnp.bfloat16), TN, preferred_element_type=jnp.float32)
            o_ref[rows, cols] = (o / total).T.astype(jnp.bfloat16)


def local_attention(q, k, v, halo_k, halo_v):
    n_rows, width = q.shape
    window = halo_k.shape[0]
    cols = 512
    row_spec = pl.BlockSpec((n_rows, cols), lambda h: (0, h))
    halo_spec = pl.BlockSpec((window, cols), lambda h: (0, h))
    elems = n_rows * 2 * window * (width // HEAD_DIM)
    return pl.pallas_call(
        functools.partial(local_kernel, window=window),
        grid=(width // cols,),
        in_specs=[row_spec, row_spec, row_spec, halo_spec, halo_spec],
        out_specs=row_spec,
        out_shape=jax.ShapeDtypeStruct((n_rows, width), jnp.bfloat16),
        scratch_shapes=[pltpu.VMEM((window + n_rows, cols), jnp.bfloat16)] * 2,
        compiler_params=pltpu.CompilerParams(vmem_limit_bytes=32 << 20),
        cost_estimate=pl.CostEstimate(flops=8 * elems * HEAD_DIM, bytes_accessed=8 * n_rows * width, transcendentals=elems),
        name="local_attention",
    )(q, k, v, halo_k, halo_v)


def solution(mesh):
    n_dev = mesh.shape['ctx']
    shift_pairs = [(src_dev, src_dev + 1) for src_dev in range(n_dev - 1)]
    row_spec = P(('dp', 'ctx'), None)
    cache_spec = P(None, ('dp', 'ctx'), None, None)
    local_spec = P(None, 'dp', None, None)
    in_specs = (row_spec, P('dp'), cache_spec, cache_spec, local_spec, local_spec) + (P(),) * 9

    def swap(x, r):
        return lax.ppermute(x, 'ctx', [(d, d ^ r) for d in range(n_dev)])

    def device_step(x_rows, cache_len, k_cache, v_cache, k_local, v_local, g_attn, g_mlp, w_q, w_k, w_v, w_o, w_gate, w_up, w_down):
        dev_idx = lax.axis_index('ctx')
        is_first = dev_idx == 0
        me = dev_idx.astype(jnp.int32).reshape(1)
        info = jnp.concatenate([me, cache_len])
        n_rows = x_rows.shape[0]
        pairs, window = k_local.shape[:2]
        width = w_q.shape[-1]
        halo_keys = k_local.reshape(pairs, window, width)
        halo_vals = v_local.reshape(pairs, window, width)
        sent = {}

        def relay_both(p):
            return relay(me, k_cache, p, n_dev), relay(me, v_cache, p, n_dev)

        def send(p, t, pieces):
            sent[p, t] = [pieces[0]] + [swap(pieces[r], r) for r in (1, 2, 3)]

        k_pieces, v_pieces = relay_both(0)
        x_rows, k_pieces = lax.optimization_barrier((x_rows, k_pieces))
        send(0, 'k', k_pieces)
        send(0, 'v', v_pieces)

        hidden = x_rows
        for p in range(pairs):
            l = 2 * p
            h = rms_norm(hidden, g_attn[l])
            k = project(h, w_k[l])
            v = project(h, w_v[l])
            halo_k = lax.ppermute(k[n_rows - window:], 'ctx', shift_pairs)
            halo_v = lax.ppermute(v[n_rows - window:], 'ctx', shift_pairs)
            q = project(h, w_q[l])
            halo_k = jnp.where(is_first, halo_keys[p], halo_k)
            halo_v = jnp.where(is_first, halo_vals[p], halo_v)
            attn = local_attention(q, k, v, halo_k, halo_v)
            hidden = (hidden.astype(jnp.float32) + jnp.dot(attn, w_o[l], preferred_element_type=jnp.float32)).astype(jnp.bfloat16)
            hidden = mlp_block(hidden, g_mlp[l], w_gate[l], w_up[l], w_down[l])

            l = 2 * p + 1
            h = rms_norm(hidden, g_attn[l])
            h1 = swap(h, 1)
            h2 = swap(h, 2)
            q_near, k_near, v_near = group_qkv(me, h, h1, w_q, w_k, w_v, l, n_dev)
            state = global_attention(info, q_near, sent[p, 'k'], sent[p, 'v'], store=True)
            h3 = swap(h2, 1)
            q_far, k_far, v_far = group_qkv(me, h2, h3, w_q, w_k, w_v, l, n_dev)
            if p + 1 < pairs:
                k_pieces, v_pieces = relay_both(p + 1)
                k_pieces, v_pieces = lax.optimization_barrier((k_pieces, v_pieces, q_far))[:2]
                send(p + 1, 'k', k_pieces)
            o2, o3 = global_attention(info, q_far, sent[p, 'k'], sent[p, 'v'], (k_near, k_far), (v_near, v_far), first=2)
            o2, o3 = swap(o2, 2), swap(o3, 3)
            if p + 1 < pairs:
                send(p + 1, 'v', v_pieces)
            o0, o1 = global_attention(info, q_near, (), (), (k_near, k_far), (v_near, v_far), state)
            o1 = swap(o1, 1)
            hidden = group_out(me, hidden, (o0, o1, o2, o3), w_o, l)
            hidden = mlp_block(hidden, g_mlp[l], w_gate[l], w_up[l], w_down[l])
        return hidden

    return jax.shard_map(device_step, mesh=mesh, in_specs=in_specs, out_specs=row_spec, check_vma=False)
```

profile of v0, /device:TPU:7, one launch (start us, length us, event | category | flops | bytes accessed | tf_op | source)
XLA Modules:
  0.0 1590.1 jit_solution(11615709809488278849)
XLA Ops:
  0.0 7.1 cache_relay.4
  9.1 10.0 fusion.176.v_ref
  21.5 9.2 fusion.173.k_ref
  33.6 10.3 fusion.170.q_ref
  51.9 20.4 %local_attention.2 = bf16[768,2048]{1,0:T(8,128)(2,1)S(1)} custom-call(bf16[768,2048]{1,0:T(8,128)(2,1)S(1)} %copy-done.26, bf16[768,2048]{1,0:T(8,128)(2,1)S(1)} %copy-done.3, bf16[768,2048]{1,0:T(8,128)(2,1)S(1)} %fusion.176.v_ref, bf16[256,2048]{1,0:T(8,128)(2,1)S(1)} %bitcast_select_fusion.3.hk_ref, bf16[256,2048]{1,0:T(8,128)(2,1)S(1)} %bitcast_select_fusion.2.hv_ref), custom_call_target="tpu_custom_call" | custom-call | flops 6442450944 | bytes 12582912 | tf_op jit(solution)/shard_map/local_attention/pallas_call | solution.py:335
  72.4 9.3 fusion.130
  81.7 33.2 %fusion.22 = f32[768,8192]{1,0:T(8,128)} fusion(bf16[4,2048,8192]{2,1,0:T(8,128)(2,1)} %param.27, bf16[768,2048]{1,0:T(8,128)(2,1)S(1)} %get-tuple-element.128, f32[2048]{0:T(1024)S(1)} %bitcast.198, f32[768]{0:T(1024)S(1)} %add_rsqrt_fusion.6), kind=kOutput, calls=%fused_computation.26 | convolution fusion | flops 25776095232 | bytes 61877248 | tf_op jit(solution)/shard_map/dot_general | solution.py:33
  114.9 38.1 %fusion.44.clone.3.clone.5 = bf16[768,8192]{1,0:T(8,128)(2,1)} fusion(f32[768,8192]{1,0:T(8,128)} %fusion.22, bf16[4,2048,8192]{2,1,0:T(8,128)(2,1)} %param.28, bf16[768,2048]{1,0:T(8,128)(2,1)S(1)} %get-tuple-element.128, f32[2048]{0:T(1024)S(1)} %bitcast.199, f32[768]{0:T(1024)S(1)} %add_rsqrt_fusion.6), kind=kOutput, calls=%fused_computation.48.clone.clone.clone.clone.clone.clone.clone.2 | convolution fusion | flops 25839009792 | bytes 74460160 | tf_op jit(solution)/shard_map/dot_general | solution.py:34
  153.0 34.4 %fusion.120 = (f32[768]{0:T(1024)S(1)}, bf16[768,2048]{1,0:T(8,128)(2,1)S(1)}) fusion(bf16[4,8192,2048]{2,1,0:T(8,128)(2,1)} %param.29, bf16[768,2048]{1,0:T(8,128)(2,1)S(1)} %get-tuple-element.128, bf16[768,8192]{1,0:T(8,128)(2,1)} %fusion.44.clone.3.clone.5), kind=kOutput, calls=%fused_computation.130 | convolution fusion | flops 25779240960 | bytes 52431872 | tf_op jit(solution)/shard_map/dot_general | solution.py:36
  206.3 34.1 %collective-permute-done.6.rest_2_ = bf16[4,2048,128]{2,1,0:T(8,128)(2,1)} collective-permute-done((bf16[4,2048,128]{2,1,0:T(8,128)(2,1)S(1)}, bf16[4,2048,128]{2,1,0:T(8,128)(2,1)}, u32[]{:S(2)}, u32[]{:S(2)}) %collective-permute-start.6) | collective-permute-done | bytes 2097184 | tf_op jit(solution)/shard_map/ppermute | solution.py:357
  246.0 15.4 group_qkv.4
  265.1 42.8 %collective-permute-done.3.h0_ref = bf16[768,2048]{1,0:T(8,128)(2,1)} collective-permute-done((bf16[768,2048]{1,0:T(8,128)(2,1)S(1)}, bf16[768,2048]{1,0:T(8,128)(2,1)}, u32[]{:S(2)}, u32[]{:S(2)}) %collective-permute-start.3) | collective-permute-done | bytes 3145760 | tf_op jit(solution)/shard_map/ppermute | solution.py:357
  310.3 44.5 %collective-permute-done.7.rest_3_ = bf16[4,2048,128]{2,1,0:T(8,128)(2,1)} collective-permute-done((bf16[4,2048,128]{2,1,0:T(8,128)(2,1)S(1)}, bf16[4,2048,128]{2,1,0:T(8,128)(2,1)}, u32[]{:S(2)}, u32[]{:S(2)}) %collective-permute-start.7) | collective-permute-done | bytes 2097184 | tf_op jit(solution)/shard_map/ppermute | solution.py:357
  354.9 44.6 %collective-permute-done.10.rest_7_ = bf16[4,2048,128]{2,1,0:T(8,128)(2,1)} collective-permute-done((bf16[4,2048,128]{2,1,0:T(8,128)(2,1)S(1)}, bf16[4,2048,128]{2,1,0:T(8,128)(2,1)}, u32[]{:S(2)}, u32[]{:S(2)}) %collective-permute-start.10) | collective-permute-done | bytes 2097184 | tf_op jit(solution)/shard_map/ppermute | solution.py:357
  399.5 43.1 %collective-permute-done.9.rest_6_ = bf16[4,2048,128]{2,1,0:T(8,128)(2,1)} collective-permute-done((bf16[4,2048,128]{2,1,0:T(8,128)(2,1)S(1)}, bf16[4,2048,128]{2,1,0:T(8,128)(2,1)}, u32[]{:S(2)}, u32[]{:S(2)}) %collective-permute-start.9) | collective-permute-done | bytes 2097184 | tf_op jit(solution)/shard_map/ppermute | solution.py:357
  442.7 60.7 %global_attention.6 = (f32[4,2,1,768]{3,2,1,0:T(1,128)}, f32[4,2,1,768]{3,2,1,0:T(1,128)}, f32[4,2,128,768]{3,2,1,0:T(8,128)}) custom-call(s32[2]{0:T(128)} %pad_add_fusion.info_ref, bf16[1536,512]{1,0:T(8,128)(2,1)} %copy-done.14, bf16[4,2048,128]{2,1,0:T(8,128)(2,1)} %copy-done.4, bf16[4,2048,128]{2,1,0:T(8,128)(2,1)} %collective-permute-done.5.rest_1_, ...), custom_call_target="tpu_custom_call" | custom-call | flops 38654705664 | bytes 16777216 | tf_op jit(solution)/shard_map/global_attention/pallas_call | solution.py:279
  505.1 15.4 group_qkv.5
  524.2 76.1 %global_attention.8 = (bf16[768,512]{1,0:T(8,128)(2,1)}, bf16[768,512]{1,0:T(8,128)(2,1)}) custom-call(s32[2]{0:T(128)} %pad_add_fusion.info_ref, bf16[1536,512]{1,0:T(8,128)(2,1)} %copy-done.24, bf16[4,2048,128]{2,1,0:T(8,128)(2,1)} %copy-done.4, bf16[4,2048,128]{2,1,0:T(8,128)(2,1)} %collective-permute-done.5.rest_1_, ...), custom_call_target="tpu_custom_call" | custom-call | flops 48318382080 | bytes 23068672 | tf_op jit(solution)/shard_map/global_attention/pallas_call | solution.py:279
  600.2 22.6 %collective-permute-start.12 = (bf16[768,512]{1,0:T(8,128)(2,1)}, bf16[768,512]{1,0:T(8,128)(2,1)S(1)}, u32[]{:S(2)}, u32[]{:S(2)}) collective-permute-start(bf16[768,512]{1,0:T(8,128)(2,1)} %get-tuple-element.84), channel_id=1, source_target_pairs={{0,2},{1,3},{2,0},{3,1},{4,6},{5,7},{6,4},{7,5}} | collective-permute-start | bytes 2359304 | tf_op jit(solution)/shard_map/ppermute | solution.py:357
  624.5 41.9 %global_attention.7 = (bf16[768,512]{1,0:T(8,128)(2,1)}, bf16[768,512]{1,0:T(8,128)(2,1)}) custom-call(s32[2]{0:T(128)} %pad_add_fusion.info_ref, bf16[1536,512]{1,0:T(8,128)(2,1)} %copy-done.14, bf16[1536,512]{1,0:T(8,128)(2,1)} %copy-done.15, bf16[1536,512]{1,0:T(8,128)(2,1)} %copy-done.22, bf16[1536,512]{1,0:T(8,128)(2,1)} %copy-done.16, ...), custom_call_target="tpu_custom_call" | custom-call | flops 9663676416 | bytes 6291456 | tf_op jit(solution)/shard_map/global_attention/pallas_call | solution.py:279
  670.1 10.2 group_out.2
  682.9 36.5 %fusion.16 = f32[768,8192]{1,0:T(8,128)} fusion(bf16[4,2048,8192]{2,1,0:T(8,128)(2,1)} %param.27, bf16[768,2048]{1,0:T(8,128)(2,1)} %group_out.2, f32[2048]{0:T(1024)S(1)} %bitcast.196, f32[768]{0:T(1024)S(1)} %add_rsqrt_fusion.4), kind=kOutput, calls=%fused_computation.20 | convolution fusion | flops 25776095232 | bytes 61877248 | tf_op jit(solution)/shard_map/dot_general | solution.py:33
  719.4 38.0 %fusion.53.clone.3.clone.5 = bf16[768,8192]{1,0:T(8,128)(2,1)} fusion(f32[768,8192]{1,0:T(8,128)} %fusion.16, bf16[4,2048,8192]{2,1,0:T(8,128)(2,1)} %param.28, bf16[768,2048]{1,0:T(8,128)(2,1)S(1)} %copy-done.29, f32[2048]{0:T(1024)S(1)} %bitcast.197, f32[768]{0:T(1024)S(1)} %add_rsqrt_fusion.4), kind=kOutput, calls=%fused_computation.57.clone.clone.clone.clone.clone.clone.clone.2 | convolution fusion | flops 25839009792 | bytes 74460160 | tf_op jit(solution)/shard_map/dot_general | solution.py:34
  757.3 34.2 %fusion.138 = (f32[768]{0:T(1024)S(1)}, bf16[768,2048]{1,0:T(8,128)(2,1)S(1)}) fusion(bf16[4,8192,2048]{2,1,0:T(8,128)(2,1)} %param.29, bf16[768,2048]{1,0:T(8,128)(2,1)S(1)} %copy-done.29, bf16[768,8192]{1,0:T(8,128)(2,1)} %fusion.53.clone.3.clone.5), kind=kOutput, calls=%fused_computation.148 | convolution fusion | flops 25779240960 | bytes 52431872 | tf_op jit(solution)/shard_map/dot_general | solution.py:36
  791.6 9.2 fusion.185.v_ref
  800.8 9.2 fusion.182.k_ref
  812.9 9.4 fusion.179.q_ref
  822.9 20.4 %local_attention.3 = bf16[768,2048]{1,0:T(8,128)(2,1)S(1)} custom-call(bf16[768,2048]{1,0:T(8,128)(2,1)S(1)} %fusion.179.q_ref, bf16[768,2048]{1,0:T(8,128)(2,1)S(1)} %fusion.182.k_ref, bf16[768,2048]{1,0:T(8,128)(2,1)S(1)} %fusion.185.v_ref, bf16[256,2048]{1,0:T(8,128)(2,1)S(1)} %bitcast_select_fusion.1.hk_ref, bf16[256,2048]{1,0:T(8,128)(2,1)S(1)} %bitcast_select_fusion.hv_ref), custom_call_target="tpu_custom_call" | custom-call | flops 6442450944 | bytes 12582912 | tf_op jit(solution)/shard_map/local_attention/pallas_call | solution.py:335
  843.4 9.5 fusion.142
  852.8 33.5 %fusion.10 = f32[768,8192]{1,0:T(8,128)} fusion(bf16[4,2048,8192]{2,1,0:T(8,128)(2,1)} %param.27, bf16[768,2048]{1,0:T(8,128)(2,1)S(1)} %get-tuple-element.134, f32[2048]{0:T(1024)S(1)} %bitcast.191, f32[768]{0:T(1024)S(1)} %add_rsqrt_fusion.2), kind=kOutput, calls=%fused_computation.14 | convolution fusion | flops 25776095232 | bytes 61877248 | tf_op jit(solution)/shard_map/dot_general | solution.py:33
  886.3 38.1 %fusion.62.clone.3.clone.5 = bf16[768,8192]{1,0:T(8,128)(2,1)} fusion(f32[768,8192]{1,0:T(8,128)} %fusion.10, bf16[4,2048,8192]{2,1,0:T(8,128)(2,1)} %param.28, bf16[768,2048]{1,0:T(8,128)(2,1)S(1)} %get-tuple-element.134, f32[2048]{0:T(1024)S(1)} %bitcast.192, f32[768]{0:T(1024)S(1)} %add_rsqrt_fusion.2), kind=kOutput, calls=%fused_computation.66.clone.clone.clone.clone.clone.clone.clone.2 | convolution fusion | flops 25839009792 | bytes 74460160 | tf_op jit(solution)/shard_map/dot_general | solution.py:34
  924.4 34.2 %fusion.123 = (f32[768]{0:T(1024)S(1)}, bf16[768,2048]{1,0:T(8,128)(2,1)S(1)}) fusion(bf16[4,8192,2048]{2,1,0:T(8,128)(2,1)} %param.29, bf16[768,2048]{1,0:T(8,128)(2,1)S(1)} %get-tuple-element.134, bf16[768,8192]{1,0:T(8,128)(2,1)} %fusion.62.clone.3.clone.5), kind=kOutput, calls=%fused_computation.133 | convolution fusion | flops 25779240960 | bytes 52431872 | tf_op jit(solution)/shard_map/dot_general | solution.py:36
  960.3 15.1 collective-permute-start.16
  997.4 43.0 %collective-permute-done.20.rest_2_ = bf16[4,2048,128]{2,1,0:T(8,128)(2,1)S(1)} collective-permute-done((bf16[4,2048,128]{2,1,0:T(8,128)(2,1)S(1)}, bf16[4,2048,128]{2,1,0:T(8,128)(2,1)S(1)}, u32[]{:S(2)}, u32[]{:S(2)}) %collective-permute-start.20) | collective-permute-done | bytes 2097184 | tf_op jit(solution)/shard_map/ppermute | solution.py:357
  1045.1 15.4 group_qkv.6
  1064.1 43.8 %collective-permute-done.17.h0_ref = bf16[768,2048]{1,0:T(8,128)(2,1)} collective-permute-done((bf16[768,2048]{1,0:T(8,128)(2,1)S(1)}, bf16[768,2048]{1,0:T(8,128)(2,1)}, u32[]{:S(2)}, u32[]{:S(2)}) %collective-permute-start.17) | collective-permute-done | bytes 3145760 | tf_op jit(solution)/shard_map/ppermute | solution.py:357
  1109.2 44.3 %collective-permute-done.21.rest_3_ = bf16[4,2048,128]{2,1,0:T(8,128)(2,1)} collective-permute-done((bf16[4,2048,128]{2,1,0:T(8,128)(2,1)S(1)}, bf16[4,2048,128]{2,1,0:T(8,128)(2,1)}, u32[]{:S(2)}, u32[]{:S(2)}) %collective-permute-start.21) | collective-permute-done | bytes 2097184 | tf_op jit(solution)/shard_map/ppermute | solution.py:357
  1153.5 44.3 %collective-permute-done.23.rest_6_ = bf16[4,2048,128]{2,1,0:T(8,128)(2,1)} collective-permute-done((bf16[4,2048,128]{2,1,0:T(8,128)(2,1)S(1)}, bf16[4,2048,128]{2,1,0:T(8,128)(2,1)}, u32[]{:S(2)}, u32[]{:S(2)}) %collective-permute-start.23) | collective-permute-done | bytes 2097184 | tf_op jit(solution)/shard_map/ppermute | solution.py:357
  1197.8 45.1 %collective-permute-done.24.rest_7_ = bf16[4,2048,128]{2,1,0:T(8,128)(2,1)} collective-permute-done((bf16[4,2048,128]{2,1,0:T(8,128)(2,1)S(1)}, bf16[4,2048,128]{2,1,0:T(8,128)(2,1)}, u32[]{:S(2)}, u32[]{:S(2)}) %collective-permute-start.24) | collective-permute-done | bytes 2097184 | tf_op jit(solution)/shard_map/ppermute | solution.py:357
  1242.9 60.7 %global_attention.9 = (f32[4,2,1,768]{3,2,1,0:T(1,128)}, f32[4,2,1,768]{3,2,1,0:T(1,128)}, f32[4,2,128,768]{3,2,1,0:T(8,128)}) custom-call(s32[2]{0:T(128)} %pad_add_fusion.info_ref, bf16[1536,512]{1,0:T(8,128)(2,1)} %copy-done.17, bf16[4,2048,128]{2,1,0:T(8,128)(2,1)} %copy-done.11, bf16[4,2048,128]{2,1,0:T(8,128)(2,1)} %copy-done.51, ...), custom_call_target="tpu_custom_call" | custom-call | flops 38654705664 | bytes 16777216 | tf_op jit(solution)/shard_map/global_attention/pallas_call | solution.py:279
  1305.4 15.4 group_qkv.7
  1324.4 76.3 %global_attention.11 = (bf16[768,512]{1,0:T(8,128)(2,1)}, bf16[768,512]{1,0:T(8,128)(2,1)}) custom-call(s32[2]{0:T(128)} %pad_add_fusion.info_ref, bf16[1536,512]{1,0:T(8,128)(2,1)} %copy-done.25, bf16[4,2048,128]{2,1,0:T(8,128)(2,1)} %copy-done.11, bf16[4,2048,128]{2,1,0:T(8,128)(2,1)} %copy-done.51, bf16[4,2048,128]{2,1,0:T(8,128)(2,1)} %copy-done.52, ...), custom_call_target="tpu_custom_call" | custom-call | flops 48318382080 | bytes 23068672 | tf_op jit(solution)/shard_map/global_attention/pallas_call | solution.py:279
  1400.7 21.6 %collective-permute-start.26 = (bf16[768,512]{1,0:T(8,128)(2,1)}, bf16[768,512]{1,0:T(8,128)(2,1)S(1)}, u32[]{:S(2)}, u32[]{:S(2)}) collective-permute-start(bf16[768,512]{1,0:T(8,128)(2,1)} %get-tuple-element.113), channel_id=1, source_target_pairs={{0,2},{1,3},{2,0},{3,1},{4,6},{5,7},{6,4},{7,5}} | collective-permute-start | bytes 2359304 | tf_op jit(solution)/shard_map/ppermute | solution.py:357
  1422.6 41.9 %global_attention.10 = (bf16[768,512]{1,0:T(8,128)(2,1)}, bf16[768,512]{1,0:T(8,128)(2,1)}) custom-call(s32[2]{0:T(128)} %pad_add_fusion.info_ref, bf16[1536,512]{1,0:T(8,128)(2,1)} %copy-done.17, bf16[1536,512]{1,0:T(8,128)(2,1)} %copy-done.18, bf16[1536,512]{1,0:T(8,128)(2,1)} %copy-done.20, bf16[1536,512]{1,0:T(8,128)(2,1)} %copy-done.19, ...), custom_call_target="tpu_custom_call" | custom-call | flops 9663676416 | bytes 6291456 | tf_op jit(solution)/shard_map/global_attention/pallas_call | solution.py:279
  1468.1 10.2 group_out.3
  1481.0 36.3 %fusion.4 = f32[768,8192]{1,0:T(8,128)} fusion(bf16[4,2048,8192]{2,1,0:T(8,128)(2,1)} %param.27, bf16[768,2048]{1,0:T(8,128)(2,1)} %group_out.3, f32[2048]{0:T(1024)S(1)} %bitcast.189, f32[768]{0:T(1024)S(1)} %add_rsqrt_fusion), kind=kOutput, calls=%fused_computation.8 | convolution fusion | flops 25776095232 | bytes 61877248 | tf_op jit(solution)/shard_map/dot_general | solution.py:33
  1517.3 38.0 %fusion.71.clone.7 = bf16[768,8192]{1,0:T(8,128)(2,1)} fusion(f32[768,8192]{1,0:T(8,128)} %fusion.4, bf16[4,2048,8192]{2,1,0:T(8,128)(2,1)} %param.28, bf16[768,2048]{1,0:T(8,128)(2,1)S(1)} %copy-done.30, f32[2048]{0:T(1024)S(1)} %bitcast.190, f32[768]{0:T(1024)S(1)} %add_rsqrt_fusion), kind=kOutput, calls=%fused_computation.75.clone.clone.clone.clone.clone.2 | convolution fusion | flops 25839009792 | bytes 74460160 | tf_op jit(solution)/shard_map/dot_general | solution.py:34
  1555.2 34.7 %fusion.149 = bf16[768,2048]{1,0:T(8,128)(2,1)} fusion(bf16[768,2048]{1,0:T(8,128)(2,1)S(1)} %copy-done.30, bf16[4,8192,2048]{2,1,0:T(8,128)(2,1)} %param.29, bf16[768,8192]{1,0:T(8,128)(2,1)} %fusion.71.clone.7), kind=kOutput, calls=%fused_computation.159 | convolution fusion | flops 25774522368 | bytes 52428800 | tf_op jit(solution)/shard_map/dot_general | solution.py:36
  (178 shorter events, 106.4 us)
Async XLA Ops:
  7.2 11.9 copy-start.4
  7.2 11.9 copy-start.5
  7.2 11.9 copy-start.7
  7.2 11.9 copy-start.9
  20.2 27.8 %collective-permute-start.1 = (bf16[256,2048]{1,0:T(8,128)(2,1)}, bf16[256,2048]{1,0:T(8,128)(2,1)}, u32[]{:S(2)}, u32[]{:S(2)}) collective-permute-start(bf16[256,2048]{1,0:T(8,128)(2,1)} %slice.149), channel_id=1, source_target_pairs={{0,1},{1,2},{2,3},{4,5},{5,6},{6,7}} | collective-permute-start | bytes 3145736 | tf_op jit(solution)/shard_map/ppermute | solution.py:389
  30.7 13.2 copy-start.2
  31.9 12.1 copy-start.41
  31.9 13.8 copy-start.42
  31.9 18.2 %collective-permute-start = (bf16[256,2048]{1,0:T(8,128)(2,1)}, bf16[256,2048]{1,0:T(8,128)(2,1)}, u32[]{:S(2)}, u32[]{:S(2)}) collective-permute-start(bf16[256,2048]{1,0:T(8,128)(2,1)} %slice.148), channel_id=1, source_target_pairs={{0,1},{1,2},{2,3},{4,5},{5,6},{6,7}} | collective-permute-start | bytes 3145736 | tf_op jit(solution)/shard_map/ppermute | solution.py:388
  51.9 20.5 %copy-start.40 = (bf16[768,2048]{1,0:T(8,128)(2,1)S(1)}, bf16[768,2048]{1,0:T(8,128)(2,1)}, u32[]{:S(2)}) copy-start(bf16[768,2048]{1,0:T(8,128)(2,1)} %param.15) | copy-start | bytes 9437188
  153.0 34.5 %copy-start.46 = (f32[1,2048]{1,0:T(1,128)S(1)}, f32[1,2048]{1,0:T(1,128)}, u32[]{:S(2)}) copy-start(f32[1,2048]{1,0:T(1,128)} %get-tuple-element.124) | copy-start | bytes 24580
  188.3 16.7 %copy-start.28 = (bf16[768,2048]{1,0:T(8,128)(2,1)}, bf16[768,2048]{1,0:T(8,128)(2,1)S(1)}, u32[]{:S(2)}) copy-start(bf16[768,2048]{1,0:T(8,128)(2,1)S(1)} %fusion.122.h0_ref) | copy-start | bytes 9437188
  188.3 54.7 %collective-permute-start.2 = (bf16[768,2048]{1,0:T(8,128)(2,1)S(1)}, bf16[768,2048]{1,0:T(8,128)(2,1)S(1)}, u32[]{:S(2)}, u32[]{:S(2)}) collective-permute-start(bf16[768,2048]{1,0:T(8,128)(2,1)S(1)} %fusion.122.h0_ref), channel_id=1, source_target_pairs={{0,1},{1,0},{2,3},{3,2},{4,5},{5,4},{6,7},{7,6}} | collective-permute-start | bytes 9437192 | tf_op jit(solution)/shard_map/ppermute | solution.py:357
  190.6 15.7 collective-permute-start.5
  192.5 47.9 %collective-permute-start.6 = (bf16[4,2048,128]{2,1,0:T(8,128)(2,1)S(1)}, bf16[4,2048,128]{2,1,0:T(8,128)(2,1)}, u32[]{:S(2)}, u32[]{:S(2)}) collective-permute-start(bf16[4,2048,128]{2,1,0:T(8,128)(2,1)S(1)} %copy-done.8), channel_id=1, source_target_pairs={{0,2},{1,3},{2,0},{3,1},{4,6},{5,7},{6,4},{7,5}} | collective-permute-start | bytes 6291464 | tf_op jit(solution)/shard_map/ppermute | solution.py:357
  195.2 112.7 %collective-permute-start.3 = (bf16[768,2048]{1,0:T(8,128)(2,1)S(1)}, bf16[768,2048]{1,0:T(8,128)(2,1)}, u32[]{:S(2)}, u32[]{:S(2)}) collective-permute-start(bf16[768,2048]{1,0:T(8,128)(2,1)S(1)} %fusion.122.h0_ref), channel_id=1, source_target_pairs={{0,2},{1,3},{2,0},{3,1},{4,6},{5,7},{6,4},{7,5}} | collective-permute-start | bytes 9437192 | tf_op jit(solution)/shard_map/ppermute | solution.py:357
  195.2 159.7 %collective-permute-start.7 = (bf16[4,2048,128]{2,1,0:T(8,128)(2,1)S(1)}, bf16[4,2048,128]{2,1,0:T(8,128)(2,1)}, u32[]{:S(2)}, u32[]{:S(2)}) collective-permute-start(bf16[4,2048,128]{2,1,0:T(8,128)(2,1)S(1)} %copy-done.6), channel_id=1, source_target_pairs={{0,3},{1,2},{2,1},{3,0},{4,7},{5,6},{6,5},{7,4}} | collective-permute-start | bytes 6291464 | tf_op jit(solution)/shard_map/ppermute | solution.py:357
  206.3 193.2 %collective-permute-start.10 = (bf16[4,2048,128]{2,1,0:T(8,128)(2,1)S(1)}, bf16[4,2048,128]{2,1,0:T(8,128)(2,1)}, u32[]{:S(2)}, u32[]{:S(2)}) collective-permute-start(bf16[4,2048,128]{2,1,0:T(8,128)(2,1)S(1)} %get-tuple-element.77), channel_id=1, source_target_pairs={{0,3},{1,2},{2,1},{3,0},{4,7},{5,6},{6,5},{7,4}} | collective-permute-start | bytes 6291464 | tf_op jit(solution)/shard_map/ppermute | solution.py:357
  240.4 159.1 %collective-permute-start.8 = (bf16[4,2048,128]{2,1,0:T(8,128)(2,1)S(1)}, bf16[4,2048,128]{2,1,0:T(8,128)(2,1)}, u32[]{:S(2)}, u32[]{:S(2)}) collective-permute-start(bf16[4,2048,128]{2,1,0:T(8,128)(2,1)S(1)} %get-tuple-element.75), channel_id=1, source_target_pairs={{0,1},{1,0},{2,3},{3,2},{4,5},{5,4},{6,7},{7,6}} | collective-permute-start | bytes 6291464 | tf_op jit(solution)/shard_map/ppermute | solution.py:357
  242.9 199.7 %collective-permute-start.9 = (bf16[4,2048,128]{2,1,0:T(8,128)(2,1)S(1)}, bf16[4,2048,128]{2,1,0:T(8,128)(2,1)}, u32[]{:S(2)}, u32[]{:S(2)}) collective-permute-start(bf16[4,2048,128]{2,1,0:T(8,128)(2,1)S(1)} %get-tuple-element.76), channel_id=1, source_target_pairs={{0,2},{1,3},{2,0},{3,1},{4,6},{5,7},{6,4},{7,5}} | collective-permute-start | bytes 6291464 | tf_op jit(solution)/shard_map/ppermute | solution.py:357
  307.9 195.5 %collective-permute-start.4 = (bf16[768,2048]{1,0:T(8,128)(2,1)}, bf16[768,2048]{1,0:T(8,128)(2,1)S(1)}, u32[]{:S(2)}, u32[]{:S(2)}) collective-permute-start(bf16[768,2048]{1,0:T(8,128)(2,1)} %collective-permute-done.3.h0_ref), channel_id=1, source_target_pairs={{0,1},{1,0},{2,3},{3,2},{4,5},{5,4},{6,7},{7,6}} | collective-permute-start | bytes 9437192 | tf_op jit(solution)/shard_map/ppermute | solution.py:357
  600.2 66.5 %collective-permute-start.12 = (bf16[768,512]{1,0:T(8,128)(2,1)}, bf16[768,512]{1,0:T(8,128)(2,1)S(1)}, u32[]{:S(2)}, u32[]{:S(2)}) collective-permute-start(bf16[768,512]{1,0:T(8,128)(2,1)} %get-tuple-element.84), channel_id=1, source_target_pairs={{0,2},{1,3},{2,0},{3,1},{4,6},{5,7},{6,4},{7,5}} | collective-permute-start | bytes 2359304 | tf_op jit(solution)/shard_map/ppermute | solution.py:357
  622.8 43.9 %collective-permute-start.13 = (bf16[768,512]{1,0:T(8,128)(2,1)}, bf16[768,512]{1,0:T(8,128)(2,1)S(1)}, u32[]{:S(2)}, u32[]{:S(2)}) collective-permute-start(bf16[768,512]{1,0:T(8,128)(2,1)} %get-tuple-element.85), channel_id=1, source_target_pairs={{0,3},{1,2},{2,1},{3,0},{4,7},{5,6},{6,5},{7,4}} | collective-permute-start | bytes 2359304 | tf_op jit(solution)/shard_map/ppermute | solution.py:357
  666.4 2.5 collective-permute-start.11
  670.1 12.8 copy-start.50
  682.9 36.5 %copy-start.29 = (bf16[768,2048]{1,0:T(8,128)(2,1)S(1)}, bf16[768,2048]{1,0:T(8,128)(2,1)}, u32[]{:S(2)}) copy-start(bf16[768,2048]{1,0:T(8,128)(2,1)} %group_out.2) | copy-start | bytes 9437188
  757.3 34.2 %copy-start.49 = (f32[1,2048]{1,0:T(1,128)S(1)}, f32[1,2048]{1,0:T(1,128)}, u32[]{:S(2)}) copy-start(f32[1,2048]{1,0:T(1,128)} %get-tuple-element.126) | copy-start | bytes 24580
  810.1 12.3 collective-permute-start.15
  811.5 10.9 copy-start.34
  811.5 11.1 copy-start.33
  811.5 11.1 collective-permute-start.14
  924.4 34.2 %copy-start.45 = (f32[1,2048]{1,0:T(1,128)S(1)}, f32[1,2048]{1,0:T(1,128)}, u32[]{:S(2)}) copy-start(f32[1,2048]{1,0:T(1,128)} %get-tuple-element.123) | copy-start | bytes 24580
  960.3 32.9 %copy-start.27 = (bf16[768,2048]{1,0:T(8,128)(2,1)}, bf16[768,2048]{1,0:T(8,128)(2,1)S(1)}, u32[]{:S(2)}) copy-start(bf16[768,2048]{1,0:T(8,128)(2,1)S(1)} %fusion.125.h0_ref) | copy-start | bytes 9437188
  960.3 80.4 %collective-permute-start.16 = (bf16[768,2048]{1,0:T(8,128)(2,1)S(1)}, bf16[768,2048]{1,0:T(8,128)(2,1)S(1)}, u32[]{:S(2)}, u32[]{:S(2)}) collective-permute-start(bf16[768,2048]{1,0:T(8,128)(2,1)S(1)} %fusion.125.h0_ref), channel_id=1, source_target_pairs={{0,1},{1,0},{2,3},{3,2},{4,5},{5,4},{6,7},{7,6}} | collective-permute-start | bytes 9437192 | tf_op jit(solution)/shard_map/ppermute | solution.py:357
  992.1 4.9 collective-permute-start.19
  993.2 47.2 %collective-permute-start.20 = (bf16[4,2048,128]{2,1,0:T(8,128)(2,1)S(1)}, bf16[4,2048,128]{2,1,0:T(8,128)(2,1)S(1)}, u32[]{:S(2)}, u32[]{:S(2)}) collective-permute-start(bf16[4,2048,128]{2,1,0:T(8,128)(2,1)S(1)} %get-tuple-element.101), channel_id=1, source_target_pairs={{0,2},{1,3},{2,0},{3,1},{4,6},{5,7},{6,4},{7,5}} | collective-permute-start | bytes 6291464 | tf_op jit(solution)/shard_map/ppermute | solution.py:357
  993.2 114.7 %collective-permute-start.17 = (bf16[768,2048]{1,0:T(8,128)(2,1)S(1)}, bf16[768,2048]{1,0:T(8,128)(2,1)}, u32[]{:S(2)}, u32[]{:S(2)}) collective-permute-start(bf16[768,2048]{1,0:T(8,128)(2,1)S(1)} %fusion.125.h0_ref), channel_id=1, source_target_pairs={{0,2},{1,3},{2,0},{3,1},{4,6},{5,7},{6,4},{7,5}} | collective-permute-start | bytes 9437192 | tf_op jit(solution)/shard_map/ppermute | solution.py:357
  994.7 158.8 %collective-permute-start.21 = (bf16[4,2048,128]{2,1,0:T(8,128)(2,1)S(1)}, bf16[4,2048,128]{2,1,0:T(8,128)(2,1)}, u32[]{:S(2)}, u32[]{:S(2)}) collective-permute-start(bf16[4,2048,128]{2,1,0:T(8,128)(2,1)S(1)} %get-tuple-element.102), channel_id=1, source_target_pairs={{0,3},{1,2},{2,1},{3,0},{4,7},{5,6},{6,5},{7,4}} | collective-permute-start | bytes 6291464 | tf_op jit(solution)/shard_map/ppermute | solution.py:357
  997.0 43.7 %copy-start.51 = (bf16[4,2048,128]{2,1,0:T(8,128)(2,1)}, bf16[4,2048,128]{2,1,0:T(8,128)(2,1)S(1)}, u32[]{:S(2)}) copy-start(bf16[4,2048,128]{2,1,0:T(8,128)(2,1)S(1)} %collective-permute-done.19.rest_1_) | copy-start | bytes 6291460
  997.0 156.5 %collective-permute-start.22 = (bf16[4,2048,128]{2,1,0:T(8,128)(2,1)S(1)}, bf16[4,2048,128]{2,1,0:T(8,128)(2,1)}, u32[]{:S(2)}, u32[]{:S(2)}) collective-permute-start(bf16[4,2048,128]{2,1,0:T(8,128)(2,1)S(1)} %get-tuple-element.104), channel_id=1, source_target_pairs={{0,1},{1,0},{2,3},{3,2},{4,5},{5,4},{6,7},{7,6}} | collective-permute-start | bytes 6291464 | tf_op jit(solution)/shard_map/ppermute | solution.py:357
  1040.4 157.4 %collective-permute-start.23 = (bf16[4,2048,128]{2,1,0:T(8,128)(2,1)S(1)}, bf16[4,2048,128]{2,1,0:T(8,128)(2,1)}, u32[]{:S(2)}, u32[]{:S(2)}) collective-permute-start(bf16[4,2048,128]{2,1,0:T(8,128)(2,1)S(1)} %get-tuple-element.105), channel_id=1, source_target_pairs={{0,2},{1,3},{2,0},{3,1},{4,6},{5,7},{6,4},{7,5}} | collective-permute-start | bytes 6291464 | tf_op jit(solution)/shard_map/ppermute | solution.py:357
  1043.5 199.5 %collective-permute-start.24 = (bf16[4,2048,128]{2,1,0:T(8,128)(2,1)S(1)}, bf16[4,2048,128]{2,1,0:T(8,128)(2,1)}, u32[]{:S(2)}, u32[]{:S(2)}) collective-permute-start(bf16[4,2048,128]{2,1,0:T(8,128)(2,1)S(1)} %get-tuple-element.106), channel_id=1, source_target_pairs={{0,3},{1,2},{2,1},{3,0},{4,7},{5,6},{6,5},{7,4}} | collective-permute-start | bytes 6291464 | tf_op jit(solution)/shard_map/ppermute | solution.py:357
  1107.9 195.8 %collective-permute-start.18 = (bf16[768,2048]{1,0:T(8,128)(2,1)}, bf16[768,2048]{1,0:T(8,128)(2,1)S(1)}, u32[]{:S(2)}, u32[]{:S(2)}) collective-permute-start(bf16[768,2048]{1,0:T(8,128)(2,1)} %collective-permute-done.17.h0_ref), channel_id=1, source_target_pairs={{0,1},{1,0},{2,3},{3,2},{4,5},{5,4},{6,7},{7,6}} | collective-permute-start | bytes 9437192 | tf_op jit(solution)/shard_map/ppermute | solution.py:357
  1400.7 64.1 %collective-permute-start.26 = (bf16[768,512]{1,0:T(8,128)(2,1)}, bf16[768,512]{1,0:T(8,128)(2,1)S(1)}, u32[]{:S(2)}, u32[]{:S(2)}) collective-permute-start(bf16[768,512]{1,0:T(8,128)(2,1)} %get-tuple-element.113), channel_id=1, source_target_pairs={{0,2},{1,3},{2,0},{3,1},{4,6},{5,7},{6,4},{7,5}} | collective-permute-start | bytes 2359304 | tf_op jit(solution)/shard_map/ppermute | solution.py:357
  1422.3 42.6 %collective-permute-start.27 = (bf16[768,512]{1,0:T(8,128)(2,1)}, bf16[768,512]{1,0:T(8,128)(2,1)S(1)}, u32[]{:S(2)}, u32[]{:S(2)}) collective-permute-start(bf16[768,512]{1,0:T(8,128)(2,1)} %get-tuple-element.114), channel_id=1, source_target_pairs={{0,3},{1,2},{2,1},{3,0},{4,7},{5,6},{6,5},{7,4}} | collective-permute-start | bytes 2359304 | tf_op jit(solution)/shard_map/ppermute | solution.py:357
  1464.5 2.5 collective-permute-start.25
  1468.1 12.8 copy-start.47
  1481.0 36.3 %copy-start.30 = (bf16[768,2048]{1,0:T(8,128)(2,1)S(1)}, bf16[768,2048]{1,0:T(8,128)(2,1)}, u32[]{:S(2)}) copy-start(bf16[768,2048]{1,0:T(8,128)(2,1)} %group_out.3) | copy-start | bytes 9437188
  (33 other events, 92.0 us)
where the time goes:
time: 1600 us; the launch traced here: 1590 us
  Pallas kernels  509 us (32%)
  matrix products  505 us (32%)
  waiting for transfers between devices  436 us (27%)
  starting transfers between devices  90.2 us (6%)
  local copies, waits for them, and re-layouts  33.9 us (2%)
    ppermute x24, waiting for transfers between devices, swap(): return lax.ppermute(x, 'ctx', [(d, d ^ r) for d in range(n_dev)])  436 us
    pallas_call x6, Pallas kernels, global_attention(): pl.pallas_call(functools.partial(global_kernel, n_dev=n_dev, slots=slots,...  358 us
    dot_general x4, matrix products, mlp_block(): up_pre = jnp.dot(normed, w_up, preferred_element_type=jnp.float32)  152 us
    dot_general x4, matrix products, mlp_block(): gate_pre = jnp.dot(normed, w_gate, preferred_element_type=jnp.float32)  139 us
    dot_general x4, matrix products, mlp_block(): jnp.dot(act_bf16, w_down, preferred_element_type=jnp.float32)  138 us
    ppermute x24, starting transfers between devices, swap(): return lax.ppermute(x, 'ctx', [(d, d ^ r) for d in range(n_dev)])  84.5 us
    pallas_call x4, Pallas kernels, group_qkv(): pl.pallas_call(qkv_kernel, grid_spec=pltpu.PrefetchScalarGridSpec(num_sca...  61.8 us
    dot_general x6, matrix products, project(): jnp.dot(rows_in, weight, preferred_element_type=jnp.float32)  57.3 us
  transfers between devices with their start and end apart: 28, of which 13 were waited for; matrix products, arithmetic and copies ran while one was open for 2% of the time, Pallas kernels for 16%

commit v1 on v0

--- a/solution.py
+++ b/solution.py
@@ -26,14 +26,6 @@
 
 def project(rows_in, weight):
     return jnp.dot(rows_in, weight, preferred_element_type=jnp.float32).astype(jnp.bfloat16)
-
-
-def mlp_block(hidden, gain_vec, w_gate, w_up, w_down):
-    normed = rms_norm(hidden, gain_vec)
-    gate_pre = jnp.dot(normed, w_gate, preferred_element_type=jnp.float32)
-    up_pre = jnp.dot(normed, w_up, preferred_element_type=jnp.float32)
-    act_bf16 = (jax.nn.gelu(gate_pre, approximate=True) * up_pre).astype(jnp.bfloat16)
-    return (hidden.astype(jnp.float32) + jnp.dot(act_bf16, w_down, preferred_element_type=jnp.float32)).astype(jnp.bfloat16)
 
 
 def relay_kernel(me_ref, x_ref, *rest):
@@ -103,36 +95,99 @@
     )(me, h0, h1, w_q, w_k, w_v)
 
 
-def out_kernel(me_ref, x_ref, o0, o1, o2, o3, w0, w1, w2, w3, y_ref):
-    total = jnp.dot(o0[...], w0[...], preferred_element_type=jnp.float32)
-    for o, w in ((o1, w1), (o2, w2), (o3, w3)):
-        total = total + jnp.dot(o[...], w[...], preferred_element_type=jnp.float32)
-    y_ref[...] = (x_ref[...].astype(jnp.float32) + total).astype(jnp.bfloat16)
-
-
-def group_out(me, x, parts, w_o, layer):
+def norm_rows(x, gain_ref):
+    inv_rms = lax.rsqrt(jnp.mean(x * x, axis=-1, keepdims=True) + NORM_EPS)
+    return (x * inv_rms * gain_ref[...].astype(jnp.float32)).astype(jnp.bfloat16)
+
+
+def mlp_kernel(me_ref, x_ref, *rest, n_parts, n_out, n_mlp, with_next):
+    rest = list(rest)
+    parts = [rest.pop(0) for _ in range(n_parts)]
+    w_parts = [rest.pop(0) for _ in range(n_parts)]
+    gain, wg_ref, wu_ref, wd_ref = [rest.pop(0) for _ in range(4)]
+    next_gain = rest.pop(0) if with_next else None
+    y_ref = rest.pop(0)
+    next_ref = rest.pop(0) if with_next else None
+    acc, h_s = rest
+    step = pl.program_id(0)
+    cols = x_ref.shape[1]
+
+    @pl.when(step < n_out)
+    def _():
+        total = x_ref[...].astype(jnp.float32)
+        attn = jnp.dot(parts[0][...], w_parts[0][...], preferred_element_type=jnp.float32)
+        for o, w in zip(parts[1:], w_parts[1:]):
+            attn = attn + jnp.dot(o[...], w[...], preferred_element_type=jnp.float32)
+        acc[:, pl.ds(pl.multiple_of(step * cols, cols), cols)] = (total + attn).astype(jnp.bfloat16).astype(jnp.float32)
+
+    @pl.when(step == n_out - 1)
+    def _():
+        h_s[...] = norm_rows(acc[...], gain)
+
+    @pl.when(step >= n_out)
+    def _():
+        h = h_s[...]
+        gate = jnp.dot(h, wg_ref[...], preferred_element_type=jnp.float32)
+        up = jnp.dot(h, wu_ref[...], preferred_element_type=jnp.float32)
+        act = (jax.nn.gelu(gate, approximate=True) * up).astype(jnp.bfloat16)
+        acc[...] += jnp.dot(act, wd_ref[...], preferred_element_type=jnp.float32)
+
+    @pl.when(step == n_out + n_mlp - 1)
+    def _():
+        y = acc[...].astype(jnp.bfloat16)
+        y_ref[...] = y
+        if with_next:
+            next_ref[...] = norm_rows(y.astype(jnp.float32), next_gain)
+
+
+def out_mlp(me, x, parts, w_o, gains, w_gate, w_up, w_down, layer, next_gains=None):
     n_rows, width = x.shape
-    group = parts[0].shape[1]
-    cols = 512
-    col_spec = pl.BlockSpec((n_rows, cols), lambda n, m: (0, n))
-    part_spec = pl.BlockSpec((n_rows, group), lambda n, m: (0, 0))
-
-    def w_spec(r):
-        return pl.BlockSpec((None, group, cols), lambda n, m: (layer, m[0] ^ r, n))
-
-    return pl.pallas_call(
-        out_kernel,
+    depth = w_gate.shape[-1]
+    cols, block = 512, 512
+    n_out, n_mlp = width // cols, depth // block
+    group = width // len(parts)
+    with_next = next_gains is not None
+
+    def out_step(i):
+        return jnp.minimum(i, n_out - 1)
+
+    def mlp_step(i):
+        return jnp.maximum(i - n_out, 0)
+
+    def part_w(r):
+        if len(parts) == 1:
+            return pl.BlockSpec((None, width, cols), lambda i, m: (layer, 0, out_step(i)))
+        return pl.BlockSpec((None, group, cols), lambda i, m: (layer, m[0] ^ r, out_step(i)))
+
+    whole = pl.BlockSpec((n_rows, width), lambda i, m: (0, 0))
+    in_specs = (
+        [pl.BlockSpec((n_rows, cols), lambda i, m: (0, out_step(i)))]
+        + [pl.BlockSpec((n_rows, group), lambda i, m: (0, 0))] * len(parts)
+        + [part_w(r) for r in range(len(parts))]
+        + [pl.BlockSpec((None, 1, width), lambda i, m: (layer, 0, 0))]
+        + [pl.BlockSpec((None, width, block), lambda i, m: (layer, 0, mlp_step(i)))] * 2
+        + [pl.BlockSpec((None, block, width), lambda i, m: (layer, mlp_step(i), 0))]
+    )
+    args = [x, *parts, *([w_o] * len(parts)), gains, w_gate, w_up, w_down]
+    if with_next:
+        in_specs.append(pl.BlockSpec((None, 1, width), lambda i, m: (layer + 1, 0, 0)))
+        args.append(next_gains)
+    n_res = 1 + with_next
+    res = pl.pallas_call(
+        functools.partial(mlp_kernel, n_parts=len(parts), n_out=n_out, n_mlp=n_mlp, with_next=with_next),
         grid_spec=pltpu.PrefetchScalarGridSpec(
             num_scalar_prefetch=1,
-            grid=(width // cols,),
-            in_specs=[col_spec] + [part_spec] * 4 + [w_spec(r) for r in range(4)],
-            out_specs=col_spec,
+            grid=(n_out + n_mlp,),
+            in_specs=in_specs,
+            out_specs=[whole] * n_res,
+            scratch_shapes=[pltpu.VMEM((n_rows, width), jnp.float32), pltpu.VMEM((n_rows, width), jnp.bfloat16)],
         ),
-        out_shape=jax.ShapeDtypeStruct((n_rows, width), jnp.bfloat16),
-        compiler_params=pltpu.CompilerParams(vmem_limit_bytes=48 << 20),
-        cost_estimate=pl.CostEstimate(flops=2 * n_rows * width * width, bytes_accessed=2 * width * width, transcendentals=0),
-        name="group_out",
-    )(me, x, *parts, *([w_o] * 4))
+        out_shape=[jax.ShapeDtypeStruct((n_rows, width), jnp.bfloat16)] * n_res,
+        compiler_params=pltpu.CompilerParams(vmem_limit_bytes=62 << 20),
+        cost_estimate=pl.CostEstimate(flops=2 * n_rows * width * (width + 3 * depth), bytes_accessed=2 * width * (width + 3 * depth), transcendentals=n_rows * depth),
+        name="out_mlp",
+    )(me, *args)
+    return res if with_next else res[0]
 
 
 def global_kernel(info_ref, q_ref, *rest, n_dev, slots, n_rows, first, use_cache, use_new, load, store):
@@ -379,10 +434,12 @@
         send(0, 'k', k_pieces)
         send(0, 'v', v_pieces)
 
+        mlp_args = (w_o, g_mlp.reshape(2 * pairs, 1, width), w_gate, w_up, w_down)
+        attn_gains = g_attn.reshape(2 * pairs, 1, width)
         hidden = x_rows
+        h = rms_norm(hidden, g_attn[0])
         for p in range(pairs):
             l = 2 * p
-            h = rms_norm(hidden, g_attn[l])
             k = project(h, w_k[l])
             v = project(h, w_v[l])
             halo_k = lax.ppermute(k[n_rows - window:], 'ctx', shift_pairs)
@@ -391,11 +448,9 @@
             halo_k = jnp.where(is_first, halo_keys[p], halo_k)
             halo_v = jnp.where(is_first, halo_vals[p], halo_v)
             attn = local_attention(q, k, v, halo_k, halo_v)
-            hidden = (hidden.astype(jnp.float32) + jnp.dot(attn, w_o[l], preferred_element_type=jnp.float32)).astype(jnp.bfloat16)
-            hidden = mlp_block(hidden, g_mlp[l], w_gate[l], w_up[l], w_down[l])
+            hidden, h = out_mlp(me, hidden, (attn,), *mlp_args, l, attn_gains)
 
             l = 2 * p + 1
-            h = rms_norm(hidden, g_attn[l])
             h1 = swap(h, 1)
             h2 = swap(h, 2)
             q_near, k_near, v_near = group_qkv(me, h, h1, w_q, w_k, w_v, l, n_dev)
@@ -412,8 +467,10 @@
                 send(p + 1, 'v', v_pieces)
             o0, o1 = global_attention(info, q_near, (), (), (k_near, k_far), (v_near, v_far), state)
             o1 = swap(o1, 1)
-            hidden = group_out(me, hidden, (o0, o1, o2, o3), w_o, l)
-            hidden = mlp_block(hidden, g_mlp[l], w_gate[l], w_up[l], w_down[l])
+            if p + 1 < pairs:
+                hidden, h = out_mlp(me, hidden, (o0, o1, o2, o3), *mlp_args, l, attn_gains)
+            else:
+                hidden = out_mlp(me, hidden, (o0, o1, o2, o3), *mlp_args, l)
         return hidden
 
     return jax.shard_map(device_step, mesh=mesh, in_specs=in_specs, out_specs=row_spec, check_vma=False)

time: 1600 us -> 1520 us (0.950)
  matrix products: 505 us -> 59.2 us
  Pallas kernels: 509 us -> 887 us
    dot_general x14 -> x0, matrix products: 448 us -> none  [the longest x4 152 us: mlp_block(): up_pre = jnp.dot(normed, w_up, preferred_element_type=jnp.float32)]
    pallas_call x2 -> x4, Pallas kernels: 20.5 us -> 398 us  [out_mlp(): pl.pallas_call(functools.partial(mlp_kernel, n_parts=len(parts), n_out=n_...]
  transfers between devices with their start and end apart: 28 -> 28, of which waited for: 13 -> 13; matrix products, arithmetic and copies ran while one was open for 2% -> 2% of each run, Pallas kernels for 16% -> 17%
where the time goes in v1:
time: 1520 us; the launch traced here: 1510 us
  Pallas kernels  887 us (58%)
  waiting for transfers between devices  436 us (29%)
  starting transfers between devices  85.4 us (6%)
  matrix products  59.2 us (4%)
  local copies, waits for them, and re-layouts  36.3 us (2%)
    ppermute x24, waiting for transfers between devices, swap(): return lax.ppermute(x, 'ctx', [(d, d ^ r) for d in range(n_dev)])  436 us
    pallas_call x4, Pallas kernels, out_mlp(): pl.pallas_call(functools.partial(mlp_kernel, n_parts=len(parts), n_out=n_...  398 us
    pallas_call x6, Pallas kernels, global_attention(): pl.pallas_call(functools.partial(global_kernel, n_dev=n_dev, slots=slots,...  357 us
    ppermute x24, starting transfers between devices, swap(): return lax.ppermute(x, 'ctx', [(d, d ^ r) for d in range(n_dev)])  79.5 us
    pallas_call x4, Pallas kernels, group_qkv(): pl.pallas_call(qkv_kernel, grid_spec=pltpu.PrefetchScalarGridSpec(num_sca...  62.7 us
    dot_general x6, matrix products, project(): jnp.dot(rows_in, weight, preferred_element_type=jnp.float32)  59.2 us
    pallas_call x2, Pallas kernels, local_attention(): pl.pallas_call(functools.partial(local_kernel, window=window), grid=(widt...  40.9 us
  transfers between devices with their start and end apart: 28, of which 13 were waited for; matrix products, arithmetic and copies ran while one was open for 2% of the time, Pallas kernels for 17%

profile of v1, /device:TPU:7, one launch (start us, length us, event | category | flops | bytes accessed | tf_op | source)
XLA Modules:
  0.0 1511.0 jit_solution(2102370801671211287)
XLA Ops:
  0.0 7.1 cache_relay.4
  7.9 11.3 fusion.27.v_ref
  21.6 9.2 fusion.24.k_ref
  35.2 10.3 fusion.21.q_ref
  46.8 2.9 fusion.42
  52.7 2.0 bitcast_select_fusion.3.hk_ref
  54.7 20.4 %local_attention.2.rest_0_ = bf16[768,2048]{1,0:T(8,128)(2,1)S(1)} custom-call(bf16[768,2048]{1,0:T(8,128)(2,1)S(1)} %copy-done.23, bf16[768,2048]{1,0:T(8,128)(2,1)S(1)} %copy-done.3, bf16[768,2048]{1,0:T(8,128)(2,1)S(1)} %fusion.27.v_ref, bf16[256,2048]{1,0:T(8,128)(2,1)S(1)} %bitcast_select_fusion.3.hk_ref, bf16[256,2048]{1,0:T(8,128)(2,1)S(1)} %bitcast_select_fusion.2.hv_ref), custom_call_target="tpu_custom_call" | custom-call | flops 6442450944 | bytes 12582912 | tf_op jit(solution)/shard_map/local_attention/pallas_call | solution.py:390
  76.8 100.0 %out_mlp.4 = (bf16[768,2048]{1,0:T(8,128)(2,1)}, bf16[768,2048]{1,0:T(8,128)(2,1)}) custom-call(s32[1]{0:T(128)} %bitcast.me_ref, bf16[768,2048]{1,0:T(8,128)(2,1)} %x_ref.5, bf16[768,2048]{1,0:T(8,128)(2,1)} %copy-done.1, bf16[4,2048,2048]{2,1,0:T(8,128)(2,1)} %rest_7_.3, bf16[4,1,2048]{2,1,0:T(2,128)(2,1)} %copy.16.rest_2_.rest_8_, ...), custom_call_target="tpu_custom_call" | custom-call | flops 83751862272 | bytes 109051904 | tf_op jit(solution)/shard_map/out_mlp/pallas_call | solution.py:176
  178.8 2.0 collective-permute-start.6
  180.7 2.4 collective-permute-start.7
  183.1 7.0 cache_relay.5
  191.5 35.0 %collective-permute-done.6.rest_2_ = bf16[4,2048,128]{2,1,0:T(8,128)(2,1)S(1)} collective-permute-done((bf16[4,2048,128]{2,1,0:T(8,128)(2,1)}, bf16[4,2048,128]{2,1,0:T(8,128)(2,1)S(1)}, u32[]{:S(2)}, u32[]{:S(2)}) %collective-permute-start.6) | collective-permute-done | bytes 2097184 | tf_op jit(solution)/shard_map/ppermute | solution.py:412
  231.2 15.6 %group_qkv.4 = (bf16[1536,512]{1,0:T(8,128)(2,1)S(1)}, bf16[1536,512]{1,0:T(8,128)(2,1)S(1)}, bf16[1536,512]{1,0:T(8,128)(2,1)S(1)}) custom-call(s32[1]{0:T(128)} %bitcast.me_ref, bf16[768,2048]{1,0:T(8,128)(2,1)} %get-tuple-element.72.h0_ref, bf16[768,2048]{1,0:T(8,128)(2,1)} %copy-done.30, bf16[4,2048,2048]{2,1,0:T(8,128)(2,1)} %wq_ref.7, ...), custom_call_target="tpu_custom_call" | custom-call | flops 9663676416 | bytes 12582912 | tf_op jit(solution)/shard_map/group_qkv/pallas_call | solution.py:83
  250.3 43.5 %collective-permute-done.3.h0_ref = bf16[768,2048]{1,0:T(8,128)(2,1)S(1)} collective-permute-done((bf16[768,2048]{1,0:T(8,128)(2,1)}, bf16[768,2048]{1,0:T(8,128)(2,1)S(1)}, u32[]{:S(2)}, u32[]{:S(2)}) %collective-permute-start.3) | collective-permute-done | bytes 3145760 | tf_op jit(solution)/shard_map/ppermute | solution.py:412
  295.6 44.6 %collective-permute-done.7.rest_3_ = bf16[4,2048,128]{2,1,0:T(8,128)(2,1)} collective-permute-done((bf16[4,2048,128]{2,1,0:T(8,128)(2,1)}, bf16[4,2048,128]{2,1,0:T(8,128)(2,1)}, u32[]{:S(2)}, u32[]{:S(2)}) %collective-permute-start.7) | collective-permute-done | bytes 2097184 | tf_op jit(solution)/shard_map/ppermute | solution.py:412
  340.2 44.6 %collective-permute-done.10.rest_7_ = bf16[4,2048,128]{2,1,0:T(8,128)(2,1)} collective-permute-done((bf16[4,2048,128]{2,1,0:T(8,128)(2,1)S(1)}, bf16[4,2048,128]{2,1,0:T(8,128)(2,1)}, u32[]{:S(2)}, u32[]{:S(2)}) %collective-permute-start.10) | collective-permute-done | bytes 2097184 | tf_op jit(solution)/shard_map/ppermute | solution.py:412
  384.9 43.9 %collective-permute-done.9.rest_6_ = bf16[4,2048,128]{2,1,0:T(8,128)(2,1)} collective-permute-done((bf16[4,2048,128]{2,1,0:T(8,128)(2,1)S(1)}, bf16[4,2048,128]{2,1,0:T(8,128)(2,1)}, u32[]{:S(2)}, u32[]{:S(2)}) %collective-permute-start.9) | collective-permute-done | bytes 2097184 | tf_op jit(solution)/shard_map/ppermute | solution.py:412
  428.8 60.5 %global_attention.6 = (f32[4,2,1,768]{3,2,1,0:T(1,128)}, f32[4,2,1,768]{3,2,1,0:T(1,128)}, f32[4,2,128,768]{3,2,1,0:T(8,128)}) custom-call(s32[2]{0:T(128)} %pad_add_fusion.info_ref, bf16[1536,512]{1,0:T(8,128)(2,1)} %copy-done.11, bf16[4,2048,128]{2,1,0:T(8,128)(2,1)} %copy-done.4, bf16[4,2048,128]{2,1,0:T(8,128)(2,1)} %copy-done.40, ...), custom_call_target="tpu_custom_call" | custom-call | flops 38654705664 | bytes 16777216 | tf_op jit(solution)/shard_map/global_attention/pallas_call | solution.py:334
  489.4 15.5 %group_qkv.5 = (bf16[1536,512]{1,0:T(8,128)(2,1)S(1)}, bf16[1536,512]{1,0:T(8,128)(2,1)S(1)}, bf16[1536,512]{1,0:T(8,128)(2,1)S(1)}) custom-call(s32[1]{0:T(128)} %bitcast.me_ref, bf16[768,2048]{1,0:T(8,128)(2,1)} %copy-done.27, bf16[768,2048]{1,0:T(8,128)(2,1)} %collective-permute-done.4.h1_ref, bf16[4,2048,2048]{2,1,0:T(8,128)(2,1)} %wq_ref.7, ...), custom_call_target="tpu_custom_call" | custom-call | flops 9663676416 | bytes 12582912 | tf_op jit(solution)/shard_map/group_qkv/pallas_call | solution.py:83
  508.4 76.1 %global_attention.8 = (bf16[768,512]{1,0:T(8,128)(2,1)}, bf16[768,512]{1,0:T(8,128)(2,1)}) custom-call(s32[2]{0:T(128)} %pad_add_fusion.info_ref, bf16[1536,512]{1,0:T(8,128)(2,1)} %copy-done.21, bf16[4,2048,128]{2,1,0:T(8,128)(2,1)} %copy-done.4, bf16[4,2048,128]{2,1,0:T(8,128)(2,1)} %copy-done.40, bf16[4,2048,128]{2,1,0:T(8,128)(2,1)} %copy-done.41, ...), custom_call_target="tpu_custom_call" | custom-call | flops 48318382080 | bytes 23068672 | tf_op jit(solution)/shard_map/global_attention/pallas_call | solution.py:334
  584.5 22.6 %collective-permute-start.12 = (bf16[768,512]{1,0:T(8,128)(2,1)}, bf16[768,512]{1,0:T(8,128)(2,1)S(1)}, u32[]{:S(2)}, u32[]{:S(2)}) collective-permute-start(bf16[768,512]{1,0:T(8,128)(2,1)} %get-tuple-element.92), channel_id=1, source_target_pairs={{0,2},{1,3},{2,0},{3,1},{4,6},{5,7},{6,4},{7,5}} | collective-permute-start | bytes 2359304 | tf_op jit(solution)/shard_map/ppermute | solution.py:412
  608.3 41.9 %global_attention.7 = (bf16[768,512]{1,0:T(8,128)(2,1)}, bf16[768,512]{1,0:T(8,128)(2,1)}) custom-call(s32[2]{0:T(128)} %pad_add_fusion.info_ref, bf16[1536,512]{1,0:T(8,128)(2,1)} %copy-done.11, bf16[1536,512]{1,0:T(8,128)(2,1)} %copy-done.12, bf16[1536,512]{1,0:T(8,128)(2,1)} %copy-done.19, bf16[1536,512]{1,0:T(8,128)(2,1)} %copy-done.13, ...), custom_call_target="tpu_custom_call" | custom-call | flops 9663676416 | bytes 6291456 | tf_op jit(solution)/shard_map/global_attention/pallas_call | solution.py:334
  650.6 2.3 collective-permute-done.11.rest_1_
  652.8 100.5 %out_mlp.5 = (bf16[768,2048]{1,0:T(8,128)(2,1)}, bf16[768,2048]{1,0:T(8,128)(2,1)}) custom-call(s32[1]{0:T(128)} %bitcast.me_ref, bf16[768,2048]{1,0:T(8,128)(2,1)} %get-tuple-element.71.x_ref, bf16[768,512]{1,0:T(8,128)(2,1)} %get-tuple-element.89.rest_0_, bf16[768,512]{1,0:T(8,128)(2,1)} %collective-permute-done.11.rest_1_, bf16[768,512]{1,0:T(8,128)(2,1)} %copy-done.34, ...), custom_call_target="tpu_custom_call" | custom-call | flops 83751862272 | bytes 109051904 | tf_op jit(solution)/shard_map/out_mlp/pallas_call | solution.py:176
  753.4 10.2 fusion.36.v_ref
  763.6 9.1 fusion.33.k_ref
  775.8 9.1 fusion.30.q_ref
  786.4 20.4 %local_attention.3.rest_0_ = bf16[768,2048]{1,0:T(8,128)(2,1)S(1)} custom-call(bf16[768,2048]{1,0:T(8,128)(2,1)S(1)} %fusion.30.q_ref, bf16[768,2048]{1,0:T(8,128)(2,1)S(1)} %fusion.33.k_ref, bf16[768,2048]{1,0:T(8,128)(2,1)S(1)} %fusion.36.v_ref, bf16[256,2048]{1,0:T(8,128)(2,1)S(1)} %bitcast_select_fusion.1.hk_ref, ...), custom_call_target="tpu_custom_call" | custom-call | flops 6442450944 | bytes 12582912 | tf_op jit(solution)/shard_map/local_attention/pallas_call | solution.py:390
  808.6 99.7 %out_mlp.6 = (bf16[768,2048]{1,0:T(8,128)(2,1)}, bf16[768,2048]{1,0:T(8,128)(2,1)}) custom-call(s32[1]{0:T(128)} %bitcast.me_ref, bf16[768,2048]{1,0:T(8,128)(2,1)} %get-tuple-element.94.x_ref, bf16[768,2048]{1,0:T(8,128)(2,1)} %copy-done, bf16[4,2048,2048]{2,1,0:T(8,128)(2,1)} %rest_7_.3, bf16[4,1,2048]{2,1,0:T(2,128)(2,1)} %copy.16.rest_2_.rest_8_, ...), custom_call_target="tpu_custom_call" | custom-call | flops 83751862272 | bytes 109051904 | tf_op jit(solution)/shard_map/out_mlp/pallas_call | solution.py:176
  908.3 14.3 collective-permute-start.16
  922.7 7.0 cache_relay.6
  931.0 7.0 cache_relay.7
  941.5 2.0 collective-permute-done.19.rest_1_
  943.6 42.4 %collective-permute-done.20.rest_2_ = bf16[4,2048,128]{2,1,0:T(8,128)(2,1)S(1)} collective-permute-done((bf16[4,2048,128]{2,1,0:T(8,128)(2,1)S(1)}, bf16[4,2048,128]{2,1,0:T(8,128)(2,1)S(1)}, u32[]{:S(2)}, u32[]{:S(2)}) %collective-permute-start.20) | collective-permute-done | bytes 2097184 | tf_op jit(solution)/shard_map/ppermute | solution.py:412
  989.0 2.6 collective-permute-start.24
  991.6 15.7 %group_qkv.6 = (bf16[1536,512]{1,0:T(8,128)(2,1)S(1)}, bf16[1536,512]{1,0:T(8,128)(2,1)S(1)}, bf16[1536,512]{1,0:T(8,128)(2,1)S(1)}) custom-call(s32[1]{0:T(128)} %bitcast.me_ref, bf16[768,2048]{1,0:T(8,128)(2,1)} %get-tuple-element.97.h0_ref, bf16[768,2048]{1,0:T(8,128)(2,1)} %copy-done.29, bf16[4,2048,2048]{2,1,0:T(8,128)(2,1)} %wq_ref.7, ...), custom_call_target="tpu_custom_call" | custom-call | flops 9663676416 | bytes 12582912 | tf_op jit(solution)/shard_map/group_qkv/pallas_call | solution.py:83
  1010.9 42.6 %collective-permute-done.17.h0_ref = bf16[768,2048]{1,0:T(8,128)(2,1)S(1)} collective-permute-done((bf16[768,2048]{1,0:T(8,128)(2,1)}, bf16[768,2048]{1,0:T(8,128)(2,1)S(1)}, u32[]{:S(2)}, u32[]{:S(2)}) %collective-permute-start.17) | collective-permute-done | bytes 3145760 | tf_op jit(solution)/shard_map/ppermute | solution.py:412
  1053.4 2.3 collective-permute-start.18
  1055.7 44.4 %collective-permute-done.21.rest_3_ = bf16[4,2048,128]{2,1,0:T(8,128)(2,1)} collective-permute-done((bf16[4,2048,128]{2,1,0:T(8,128)(2,1)S(1)}, bf16[4,2048,128]{2,1,0:T(8,128)(2,1)}, u32[]{:S(2)}, u32[]{:S(2)}) %collective-permute-start.21) | collective-permute-done | bytes 2097184 | tf_op jit(solution)/shard_map/ppermute | solution.py:412
  1100.1 43.3 %collective-permute-done.23.rest_6_ = bf16[4,2048,128]{2,1,0:T(8,128)(2,1)} collective-permute-done((bf16[4,2048,128]{2,1,0:T(8,128)(2,1)S(1)}, bf16[4,2048,128]{2,1,0:T(8,128)(2,1)}, u32[]{:S(2)}, u32[]{:S(2)}) %collective-permute-start.23) | collective-permute-done | bytes 2097184 | tf_op jit(solution)/shard_map/ppermute | solution.py:412
  1143.4 45.6 %collective-permute-done.24.rest_7_ = bf16[4,2048,128]{2,1,0:T(8,128)(2,1)} collective-permute-done((bf16[4,2048,128]{2,1,0:T(8,128)(2,1)S(1)}, bf16[4,2048,128]{2,1,0:T(8,128)(2,1)}, u32[]{:S(2)}, u32[]{:S(2)}) %collective-permute-start.24) | collective-permute-done | bytes 2097184 | tf_op jit(solution)/shard_map/ppermute | solution.py:412
  1189.0 60.5 %global_attention.9 = (f32[4,2,1,768]{3,2,1,0:T(1,128)}, f32[4,2,1,768]{3,2,1,0:T(1,128)}, f32[4,2,128,768]{3,2,1,0:T(8,128)}) custom-call(s32[2]{0:T(128)} %pad_add_fusion.info_ref, bf16[1536,512]{1,0:T(8,128)(2,1)} %copy-done.14, bf16[4,2048,128]{2,1,0:T(8,128)(2,1)} %copy-done.6, bf16[4,2048,128]{2,1,0:T(8,128)(2,1)} %copy-done.42, ...), custom_call_target="tpu_custom_call" | custom-call | flops 38654705664 | bytes 16777216 | tf_op jit(solution)/shard_map/global_attention/pallas_call | solution.py:334
  1251.4 15.9 %group_qkv.7 = (bf16[1536,512]{1,0:T(8,128)(2,1)S(1)}, bf16[1536,512]{1,0:T(8,128)(2,1)S(1)}, bf16[1536,512]{1,0:T(8,128)(2,1)S(1)}) custom-call(s32[1]{0:T(128)} %bitcast.me_ref, bf16[768,2048]{1,0:T(8,128)(2,1)} %copy-done.28, bf16[768,2048]{1,0:T(8,128)(2,1)} %copy-done.31, bf16[4,2048,2048]{2,1,0:T(8,128)(2,1)} %wq_ref.7, bf16[4,2048,2048]{2,1,0:T(8,128)(2,1)} %wk_ref.7, ...), custom_call_target="tpu_custom_call" | custom-call | flops 9663676416 | bytes 12582912 | tf_op jit(solution)/shard_map/group_qkv/pallas_call | solution.py:83
  1270.8 75.8 %global_attention.11 = (bf16[768,512]{1,0:T(8,128)(2,1)}, bf16[768,512]{1,0:T(8,128)(2,1)}) custom-call(s32[2]{0:T(128)} %pad_add_fusion.info_ref, bf16[1536,512]{1,0:T(8,128)(2,1)} %copy-done.22, bf16[4,2048,128]{2,1,0:T(8,128)(2,1)} %copy-done.6, bf16[4,2048,128]{2,1,0:T(8,128)(2,1)} %copy-done.42, bf16[4,2048,128]{2,1,0:T(8,128)(2,1)} %copy-done.43, ...), custom_call_target="tpu_custom_call" | custom-call | flops 48318382080 | bytes 23068672 | tf_op jit(solution)/shard_map/global_attention/pallas_call | solution.py:334
  1346.6 21.4 %collective-permute-start.26 = (bf16[768,512]{1,0:T(8,128)(2,1)}, bf16[768,512]{1,0:T(8,128)(2,1)S(1)}, u32[]{:S(2)}, u32[]{:S(2)}) collective-permute-start(bf16[768,512]{1,0:T(8,128)(2,1)} %get-tuple-element.125), channel_id=1, source_target_pairs={{0,2},{1,3},{2,0},{3,1},{4,6},{5,7},{6,4},{7,5}} | collective-permute-start | bytes 2359304 | tf_op jit(solution)/shard_map/ppermute | solution.py:412
  1368.1 42.0 %global_attention.10 = (bf16[768,512]{1,0:T(8,128)(2,1)}, bf16[768,512]{1,0:T(8,128)(2,1)}) custom-call(s32[2]{0:T(128)} %pad_add_fusion.info_ref, bf16[1536,512]{1,0:T(8,128)(2,1)} %copy-done.14, bf16[1536,512]{1,0:T(8,128)(2,1)} %copy-done.15, bf16[1536,512]{1,0:T(8,128)(2,1)} %copy-done.17, bf16[1536,512]{1,0:T(8,128)(2,1)} %copy-done.16, ...), custom_call_target="tpu_custom_call" | custom-call | flops 9663676416 | bytes 6291456 | tf_op jit(solution)/shard_map/global_attention/pallas_call | solution.py:334
  1410.5 2.2 collective-permute-done.25.rest_1_
  1412.8 98.1 %out_mlp.7 = bf16[768,2048]{1,0:T(8,128)(2,1)} custom-call(s32[1]{0:T(128)} %bitcast.me_ref, bf16[768,2048]{1,0:T(8,128)(2,1)} %get-tuple-element.96.x_ref, bf16[768,512]{1,0:T(8,128)(2,1)} %get-tuple-element.122.rest_0_, bf16[768,512]{1,0:T(8,128)(2,1)} %collective-permute-done.25.rest_1_, bf16[768,512]{1,0:T(8,128)(2,1)} %copy-done.33, ...), custom_call_target="tpu_custom_call" | custom-call | flops 83751862272 | bytes 109051904 | tf_op jit(solution)/shard_map/out_mlp/pallas_call | solution.py:176
  (138 shorter events, 54.6 us)
Async XLA Ops:
  0.0 7.2 copy-start.24
  7.2 12.1 copy-start.4
  7.2 12.1 copy-start.5
  7.2 12.1 copy-start.7
  7.2 12.1 copy-start.9
  20.3 30.7 %collective-permute-start.1 = (bf16[256,2048]{1,0:T(8,128)(2,1)}, bf16[256,2048]{1,0:T(8,128)(2,1)}, u32[]{:S(2)}, u32[]{:S(2)}) collective-permute-start(bf16[256,2048]{1,0:T(8,128)(2,1)} %slice.65), channel_id=1, source_target_pairs={{0,1},{1,2},{2,3},{4,5},{5,6},{6,7}} | collective-permute-start | bytes 3145736 | tf_op jit(solution)/shard_map/ppermute | solution.py:446
  33.5 12.0 copy-start.38
  33.5 19.1 %collective-permute-start = (bf16[256,2048]{1,0:T(8,128)(2,1)}, bf16[256,2048]{1,0:T(8,128)(2,1)}, u32[]{:S(2)}, u32[]{:S(2)}) collective-permute-start(bf16[256,2048]{1,0:T(8,128)(2,1)} %slice.64), channel_id=1, source_target_pairs={{0,1},{1,2},{2,3},{4,5},{5,6},{6,7}} | collective-permute-start | bytes 3145736 | tf_op jit(solution)/shard_map/ppermute | solution.py:445
  45.5 4.2 copy-start.32
  51.0 3.6 copy-start.3
  51.0 3.6 copy-start.23
  176.8 51.4 %collective-permute-start.2 = (bf16[768,2048]{1,0:T(8,128)(2,1)}, bf16[768,2048]{1,0:T(8,128)(2,1)S(1)}, u32[]{:S(2)}, u32[]{:S(2)}) collective-permute-start(bf16[768,2048]{1,0:T(8,128)(2,1)} %get-tuple-element.72.h0_ref), channel_id=1, source_target_pairs={{0,1},{1,0},{2,3},{3,2},{4,5},{5,4},{6,7},{7,6}} | collective-permute-start | bytes 9437192 | tf_op jit(solution)/shard_map/ppermute | solution.py:412
  178.7 12.7 collective-permute-start.5
  178.8 47.7 %collective-permute-start.6 = (bf16[4,2048,128]{2,1,0:T(8,128)(2,1)}, bf16[4,2048,128]{2,1,0:T(8,128)(2,1)S(1)}, u32[]{:S(2)}, u32[]{:S(2)}) collective-permute-start(bf16[4,2048,128]{2,1,0:T(8,128)(2,1)} %copy-done.7), channel_id=1, source_target_pairs={{0,2},{1,3},{2,0},{3,1},{4,6},{5,7},{6,4},{7,5}} | collective-permute-start | bytes 6291464 | tf_op jit(solution)/shard_map/ppermute | solution.py:412
  180.7 113.1 %collective-permute-start.3 = (bf16[768,2048]{1,0:T(8,128)(2,1)}, bf16[768,2048]{1,0:T(8,128)(2,1)S(1)}, u32[]{:S(2)}, u32[]{:S(2)}) collective-permute-start(bf16[768,2048]{1,0:T(8,128)(2,1)} %get-tuple-element.72.h0_ref), channel_id=1, source_target_pairs={{0,2},{1,3},{2,0},{3,1},{4,6},{5,7},{6,4},{7,5}} | collective-permute-start | bytes 9437192 | tf_op jit(solution)/shard_map/ppermute | solution.py:412
  180.7 159.5 %collective-permute-start.7 = (bf16[4,2048,128]{2,1,0:T(8,128)(2,1)}, bf16[4,2048,128]{2,1,0:T(8,128)(2,1)}, u32[]{:S(2)}, u32[]{:S(2)}) collective-permute-start(bf16[4,2048,128]{2,1,0:T(8,128)(2,1)} %copy-done.5), channel_id=1, source_target_pairs={{0,3},{1,2},{2,1},{3,0},{4,7},{5,6},{6,5},{7,4}} | collective-permute-start | bytes 6291464 | tf_op jit(solution)/shard_map/ppermute | solution.py:412
  191.5 55.4 %copy-start.40 = (bf16[4,2048,128]{2,1,0:T(8,128)(2,1)}, bf16[4,2048,128]{2,1,0:T(8,128)(2,1)S(1)}, u32[]{:S(2)}) copy-start(bf16[4,2048,128]{2,1,0:T(8,128)(2,1)S(1)} %collective-permute-done.5.rest_1_) | copy-start | bytes 6291460
  191.5 193.4 %collective-permute-start.10 = (bf16[4,2048,128]{2,1,0:T(8,128)(2,1)S(1)}, bf16[4,2048,128]{2,1,0:T(8,128)(2,1)}, u32[]{:S(2)}, u32[]{:S(2)}) collective-permute-start(bf16[4,2048,128]{2,1,0:T(8,128)(2,1)S(1)} %get-tuple-element.85), channel_id=1, source_target_pairs={{0,3},{1,2},{2,1},{3,0},{4,7},{5,6},{6,5},{7,4}} | collective-permute-start | bytes 6291464 | tf_op jit(solution)/shard_map/ppermute | solution.py:412
  226.4 4.1 copy-start.41
  226.4 158.5 %collective-permute-start.8 = (bf16[4,2048,128]{2,1,0:T(8,128)(2,1)S(1)}, bf16[4,2048,128]{2,1,0:T(8,128)(2,1)}, u32[]{:S(2)}, u32[]{:S(2)}) collective-permute-start(bf16[4,2048,128]{2,1,0:T(8,128)(2,1)S(1)} %get-tuple-element.83), channel_id=1, source_target_pairs={{0,1},{1,0},{2,3},{3,2},{4,5},{5,4},{6,7},{7,6}} | collective-permute-start | bytes 6291464 | tf_op jit(solution)/shard_map/ppermute | solution.py:412
  228.2 2.4 copy-start.30
  228.2 200.6 %collective-permute-start.9 = (bf16[4,2048,128]{2,1,0:T(8,128)(2,1)S(1)}, bf16[4,2048,128]{2,1,0:T(8,128)(2,1)}, u32[]{:S(2)}, u32[]{:S(2)}) collective-permute-start(bf16[4,2048,128]{2,1,0:T(8,128)(2,1)S(1)} %get-tuple-element.84), channel_id=1, source_target_pairs={{0,2},{1,3},{2,0},{3,1},{4,6},{5,7},{6,4},{7,5}} | collective-permute-start | bytes 6291464 | tf_op jit(solution)/shard_map/ppermute | solution.py:412
  293.9 195.5 %copy-start.27 = (bf16[768,2048]{1,0:T(8,128)(2,1)}, bf16[768,2048]{1,0:T(8,128)(2,1)S(1)}, u32[]{:S(2)}) copy-start(bf16[768,2048]{1,0:T(8,128)(2,1)S(1)} %collective-permute-done.3.h0_ref) | copy-start | bytes 9437188
  293.9 195.5 %collective-permute-start.4 = (bf16[768,2048]{1,0:T(8,128)(2,1)S(1)}, bf16[768,2048]{1,0:T(8,128)(2,1)}, u32[]{:S(2)}, u32[]{:S(2)}) collective-permute-start(bf16[768,2048]{1,0:T(8,128)(2,1)S(1)} %collective-permute-done.3.h0_ref), channel_id=1, source_target_pairs={{0,1},{1,0},{2,3},{3,2},{4,5},{5,4},{6,7},{7,6}} | collective-permute-start | bytes 9437192 | tf_op jit(solution)/shard_map/ppermute | solution.py:412
  584.5 66.1 %collective-permute-start.12 = (bf16[768,512]{1,0:T(8,128)(2,1)}, bf16[768,512]{1,0:T(8,128)(2,1)S(1)}, u32[]{:S(2)}, u32[]{:S(2)}) collective-permute-start(bf16[768,512]{1,0:T(8,128)(2,1)} %get-tuple-element.92), channel_id=1, source_target_pairs={{0,2},{1,3},{2,0},{3,1},{4,6},{5,7},{6,4},{7,5}} | collective-permute-start | bytes 2359304 | tf_op jit(solution)/shard_map/ppermute | solution.py:412
  607.0 43.5 %collective-permute-start.13 = (bf16[768,512]{1,0:T(8,128)(2,1)}, bf16[768,512]{1,0:T(8,128)(2,1)S(1)}, u32[]{:S(2)}, u32[]{:S(2)}) collective-permute-start(bf16[768,512]{1,0:T(8,128)(2,1)} %get-tuple-element.93), channel_id=1, source_target_pairs={{0,3},{1,2},{2,1},{3,0},{4,7},{5,6},{6,5},{7,4}} | collective-permute-start | bytes 2359304 | tf_op jit(solution)/shard_map/ppermute | solution.py:412
  650.2 2.6 collective-permute-start.11
  650.5 2.3 copy-start.34
  650.6 2.3 copy-start.36
  753.4 10.2 copy-start.39
  772.8 12.1 collective-permute-start.15
  774.2 10.8 copy-start.26
  774.2 11.0 collective-permute-start.14
  908.3 78.0 %collective-permute-start.16 = (bf16[768,2048]{1,0:T(8,128)(2,1)}, bf16[768,2048]{1,0:T(8,128)(2,1)S(1)}, u32[]{:S(2)}, u32[]{:S(2)}) collective-permute-start(bf16[768,2048]{1,0:T(8,128)(2,1)} %get-tuple-element.97.h0_ref), channel_id=1, source_target_pairs={{0,1},{1,0},{2,3},{3,2},{4,5},{5,4},{6,7},{7,6}} | collective-permute-start | bytes 9437192 | tf_op jit(solution)/shard_map/ppermute | solution.py:412
  939.3 4.2 collective-permute-start.19
  939.3 46.7 %collective-permute-start.20 = (bf16[4,2048,128]{2,1,0:T(8,128)(2,1)S(1)}, bf16[4,2048,128]{2,1,0:T(8,128)(2,1)S(1)}, u32[]{:S(2)}, u32[]{:S(2)}) collective-permute-start(bf16[4,2048,128]{2,1,0:T(8,128)(2,1)S(1)} %get-tuple-element.113), channel_id=1, source_target_pairs={{0,2},{1,3},{2,0},{3,1},{4,6},{5,7},{6,4},{7,5}} | collective-permute-start | bytes 6291464 | tf_op jit(solution)/shard_map/ppermute | solution.py:412
  939.3 114.1 %collective-permute-start.17 = (bf16[768,2048]{1,0:T(8,128)(2,1)}, bf16[768,2048]{1,0:T(8,128)(2,1)S(1)}, u32[]{:S(2)}, u32[]{:S(2)}) collective-permute-start(bf16[768,2048]{1,0:T(8,128)(2,1)} %get-tuple-element.97.h0_ref), channel_id=1, source_target_pairs={{0,2},{1,3},{2,0},{3,1},{4,6},{5,7},{6,4},{7,5}} | collective-permute-start | bytes 9437192 | tf_op jit(solution)/shard_map/ppermute | solution.py:412
  940.8 159.3 %collective-permute-start.21 = (bf16[4,2048,128]{2,1,0:T(8,128)(2,1)S(1)}, bf16[4,2048,128]{2,1,0:T(8,128)(2,1)}, u32[]{:S(2)}, u32[]{:S(2)}) collective-permute-start(bf16[4,2048,128]{2,1,0:T(8,128)(2,1)S(1)} %get-tuple-element.114), channel_id=1, source_target_pairs={{0,3},{1,2},{2,1},{3,0},{4,7},{5,6},{6,5},{7,4}} | collective-permute-start | bytes 6291464 | tf_op jit(solution)/shard_map/ppermute | solution.py:412
  943.5 42.8 %copy-start.42 = (bf16[4,2048,128]{2,1,0:T(8,128)(2,1)}, bf16[4,2048,128]{2,1,0:T(8,128)(2,1)S(1)}, u32[]{:S(2)}) copy-start(bf16[4,2048,128]{2,1,0:T(8,128)(2,1)S(1)} %collective-permute-done.19.rest_1_) | copy-start | bytes 6291460
  943.5 156.6 %collective-permute-start.22 = (bf16[4,2048,128]{2,1,0:T(8,128)(2,1)S(1)}, bf16[4,2048,128]{2,1,0:T(8,128)(2,1)}, u32[]{:S(2)}, u32[]{:S(2)}) collective-permute-start(bf16[4,2048,128]{2,1,0:T(8,128)(2,1)S(1)} %get-tuple-element.116), channel_id=1, source_target_pairs={{0,1},{1,0},{2,3},{3,2},{4,5},{5,4},{6,7},{7,6}} | collective-permute-start | bytes 6291464 | tf_op jit(solution)/shard_map/ppermute | solution.py:412
  986.0 157.4 %collective-permute-start.23 = (bf16[4,2048,128]{2,1,0:T(8,128)(2,1)S(1)}, bf16[4,2048,128]{2,1,0:T(8,128)(2,1)}, u32[]{:S(2)}, u32[]{:S(2)}) collective-permute-start(bf16[4,2048,128]{2,1,0:T(8,128)(2,1)S(1)} %get-tuple-element.117), channel_id=1, source_target_pairs={{0,2},{1,3},{2,0},{3,1},{4,6},{5,7},{6,4},{7,5}} | collective-permute-start | bytes 6291464 | tf_op jit(solution)/shard_map/ppermute | solution.py:412
  989.0 200.0 %collective-permute-start.24 = (bf16[4,2048,128]{2,1,0:T(8,128)(2,1)S(1)}, bf16[4,2048,128]{2,1,0:T(8,128)(2,1)}, u32[]{:S(2)}, u32[]{:S(2)}) collective-permute-start(bf16[4,2048,128]{2,1,0:T(8,128)(2,1)S(1)} %get-tuple-element.118), channel_id=1, source_target_pairs={{0,3},{1,2},{2,1},{3,0},{4,7},{5,6},{6,5},{7,4}} | collective-permute-start | bytes 6291464 | tf_op jit(solution)/shard_map/ppermute | solution.py:412
  1053.4 196.2 %copy-start.28 = (bf16[768,2048]{1,0:T(8,128)(2,1)}, bf16[768,2048]{1,0:T(8,128)(2,1)S(1)}, u32[]{:S(2)}) copy-start(bf16[768,2048]{1,0:T(8,128)(2,1)S(1)} %collective-permute-done.17.h0_ref) | copy-start | bytes 9437188
  1053.4 196.2 %collective-permute-start.18 = (bf16[768,2048]{1,0:T(8,128)(2,1)S(1)}, bf16[768,2048]{1,0:T(8,128)(2,1)S(1)}, u32[]{:S(2)}, u32[]{:S(2)}) collective-permute-start(bf16[768,2048]{1,0:T(8,128)(2,1)S(1)} %collective-permute-done.17.h0_ref), channel_id=1, source_target_pairs={{0,1},{1,0},{2,3},{3,2},{4,5},{5,4},{6,7},{7,6}} | collective-permute-start | bytes 9437192 | tf_op jit(solution)/shard_map/ppermute | solution.py:412
  1346.6 63.9 %collective-permute-start.26 = (bf16[768,512]{1,0:T(8,128)(2,1)}, bf16[768,512]{1,0:T(8,128)(2,1)S(1)}, u32[]{:S(2)}, u32[]{:S(2)}) collective-permute-start(bf16[768,512]{1,0:T(8,128)(2,1)} %get-tuple-element.125), channel_id=1, source_target_pairs={{0,2},{1,3},{2,0},{3,1},{4,6},{5,7},{6,4},{7,5}} | collective-permute-start | bytes 2359304 | tf_op jit(solution)/shard_map/ppermute | solution.py:412
  1368.1 42.5 %collective-permute-start.27 = (bf16[768,512]{1,0:T(8,128)(2,1)}, bf16[768,512]{1,0:T(8,128)(2,1)S(1)}, u32[]{:S(2)}, u32[]{:S(2)}) collective-permute-start(bf16[768,512]{1,0:T(8,128)(2,1)} %get-tuple-element.126), channel_id=1, source_target_pairs={{0,3},{1,2},{2,1},{3,0},{4,7},{5,6},{6,5},{7,4}} | collective-permute-start | bytes 2359304 | tf_op jit(solution)/shard_map/ppermute | solution.py:412
  1410.1 2.7 collective-permute-start.25
  1410.5 2.3 copy-start.33
  (24 other events, 32.0 us)
